TPU v7x, 32 devices: a whole 2x2x4 slice. The times are simulated.
32 devices in a mesh: groups: 2 (over y), seq: 4 (over z), sample: 2 (over x), vocab: 2 (over core).
Axes of the slice: x: 2, y: 2, z: 4, core: 2. Of those that a mesh axis runs over, the one named last changes fastest.
Arguments:
- queries: bfloat16 [16, 256, 1792], P(('groups', 'sample'), 'seq', 'vocab'), parts along dimension 0, may hold values from -130 to 130
- key_states: bfloat16 [16, 256, 256], P(('groups', 'sample'), 'seq', 'vocab'), parts along dimension 0, may hold values from -8 to 8
- value_states: bfloat16 [16, 256, 256], P(('groups', 'sample'), 'seq', 'vocab'), parts along dimension 0, may hold values from -6 to 6
- residual: bfloat16 [16, 256, 1792], P(('groups', 'sample'), 'seq'), parts along dimension 0, may hold values from -3 to 3
- out_weight: bfloat16 [1792, 1792], P('vocab'), may hold values from -0.5 to 0.5
- norm_gain: float32 [1792], replicated, may hold values from 0.5 to 1.5
- vocab_head: bfloat16 [81920, 1792], P(('seq', 'sample', 'vocab')), may hold values from -21 to 21
- targets: int32 [16, 256], P(('groups', 'sample')), parts along dimension 0, may hold values from 0 to 81919
- scored_slots: int32 [16, 64], P(('groups', 'sample')), parts along dimension 0, may hold values from -1 to 255, as said below
- lengths: int32 [16], P(('groups', 'sample')), parts along dimension 0, may hold values from 64 to 256
- rewards: int32 [16], P(('groups', 'sample')), parts along dimension 0, may hold values from 0 to 4
Outputs:
- token_logprobs: float32 [16, 64], P(('groups', 'sample'), 'seq'), parts along dimension 0
- seq_scores: float32 [16], P(('groups', 'sample')), parts along dimension 0
- advantages: float32 [16], P(('groups', 'sample')), parts along dimension 0
- objective: float32 [2], P('groups'), parts along dimension 0
There are 2 independent parts, one for each index of `groups`. A program takes and returns all parts, laid end to end along the dimension named above; an argument that names none is the same for every part. Nothing has to cross between parts.
Inputs may be any that keep to these rules, and one draw needn't show every extreme that they name: `scored_slots`: slots b * 16 to (b + 1) * 16 - 1 of a completion hold distinct positions of b * 64 to (b + 1) * 64 - 1 in rising order, followed by -1 in unused slots; every completion fills all 16 slots of some block; positions not listed are not scored. Positions from lengths[i] on are padding.
All inputs are finite; a program needn't handle non-finite values.
Results may differ from a plain program's by a relative error of at most 0.0085.
Values may be sent and summed in bfloat16 or wider, within the bound.
No kernel may reach another device: no remote copies, remote signals or barrier semaphores. Data moves between devices by JAX's collectives and lax.ppermute only.
A program may use at most 128 MiB of HBM per device.

v0:
```python
import functools

import jax
import jax.numpy as jnp
from jax import lax
from jax.experimental import pallas as pl
from jax.experimental.pallas import tpu as pltpu
from jax.sharding import PartitionSpec as P


HD = 128
F32 = jnp.float32
BF16 = jnp.bfloat16
FLOOR = -1e30
CELL = ("seq", "sample", "vocab")


def vmem():
    return pl.BlockSpec(memory_space=pltpu.VMEM)


def hbm():
    return pl.BlockSpec(memory_space=pltpu.HBM)


def keep(array):
    return pltpu.with_memory_space_constraint(array, pltpu.HBM)


def smem():
    return pl.BlockSpec(memory_space=pltpu.SMEM)


def call(body, outs, ins, in_specs, out_specs=None, scratch=(), limit=12, flops=None):
    cost = None
    if flops is not None:
        cost = pl.CostEstimate(flops=flops, bytes_accessed=0, transcendentals=0)
    return pl.pallas_call(
        body,
        cost_estimate=cost,
        out_shape=outs,
        in_specs=in_specs,
        out_specs=jax.tree.map(lambda _: vmem(), outs) if out_specs is None else out_specs,
        scratch_shapes=list(scratch),
        compiler_params=pltpu.CompilerParams(vmem_limit_bytes=limit * 2**20),
    )(*ins)


def iota(shape, dim):
    return lax.broadcasted_iota(jnp.int32, shape, dim)


def own_slot_column(slots_row, seq_at, cap):
    total = slots_row.shape[1]
    hit = iota((cap, total), 1) == iota((cap, total), 0) + seq_at * cap
    return jnp.sum(jnp.where(hit, slots_row, 0), axis=1, keepdims=True)


def pack_kernel(keys, values, out, sems):
    width = keys.shape[2]
    copies = [
        pltpu.make_async_copy(ref, out.at[:, :, pl.ds(n * width, width)], sems.at[n])
        for n, ref in enumerate((keys, values))
    ]
    for copy in copies:
        copy.start()
    for copy in copies:
        copy.wait()


def prep_kernel(
    count, slots_in, targets_in, lengths_in, rewards_in, queries, residual, weight, gain, head,
    slots, q_out, r_out, meta_out, weight_out, gain_out, head_out,
    targets, lengths, rewards, q_in, r_in, sems,
):
    samples, block, width = queries.shape
    total, length = slots.shape[1], targets.shape[1]
    heads = width // HD
    cap = r_out.shape[0] // samples
    seq_at = lax.axis_index("seq")
    lanes = meta_out.shape[1]
    step = head.shape[0] // count
    moves = [
        (slots_in, slots), (targets_in, targets), (lengths_in, lengths), (rewards_in, rewards),
        (queries, q_in), (residual, r_in), (weight, weight_out), (gain, gain_out),
    ]
    for n in range(count):
        moves.append((head.at[pl.ds(n * step, step), :], head_out.at[pl.ds(n * step, step), :]))
    copies = [pltpu.make_async_copy(a, b, sems.at[n]) for n, (a, b) in enumerate(moves)]
    for copy in copies:
        copy.start()
    for copy in copies[:4]:
        copy.wait()
    reward_row = jnp.zeros((1, lanes), jnp.int32)
    onehots = []
    for i in range(samples):
        row = slots[i : i + 1, :]
        local = jnp.clip(own_slot_column(row, seq_at, cap) - seq_at * block, 0, block - 1)
        onehots.append((iota((cap, block), 1) == local).astype(F32).astype(BF16))
        eye = iota((total, total), 0) == iota((total, total), 1)
        column = jnp.sum(jnp.where(eye, jnp.maximum(row, 0), 0), axis=1, keepdims=True)
        spot = iota((total, length), 1) == column
        found = jnp.sum(jnp.where(spot, targets[i : i + 1, :], 0), axis=1, keepdims=True)
        wanted = jnp.sum(jnp.where(eye, found, 0), axis=0, keepdims=True)
        wanted = jnp.where((row >= 0) & (row < lengths[i]), wanted, -1)
        for n in range(total // cap):
            meta_out[n : n + 1, i * cap : (i + 1) * cap] = wanted[:, n * cap : (n + 1) * cap]
        reward_row = jnp.where(iota((1, lanes), 1) == i, rewards[i], reward_row)
    meta_out[total // cap : total // cap + 1, :] = reward_row
    copies[4].wait()
    for i in range(samples):
        picked = jnp.dot(onehots[i], q_in[i], preferred_element_type=F32).astype(BF16)
        for h in range(heads):
            q_out[i, h * cap : (h + 1) * cap, :] = picked[:, h * HD : (h + 1) * HD]
    copies[5].wait()
    for i in range(samples):
        r_out[i * cap : (i + 1) * cap, :] = jnp.dot(
            onehots[i], r_in[i], preferred_element_type=F32
        ).astype(BF16)
    for copy in copies[6:]:
        copy.wait()


def attend_kernel(offsets, slots, queries, weight, *refs):
    blocks, out = refs[:-1], refs[-1]
    samples, stacked, _ = queries.shape
    block_len, kv_width = blocks[0].shape[1], blocks[0].shape[2]
    kv_heads = kv_width // (2 * HD)
    heads = weight.shape[0] // HD
    cap = stacked // heads
    group = heads // kv_heads
    span = block_len * len(blocks)
    seq_at = lax.axis_index("seq")
    lane = iota((1, span), 1)
    key_pos = lane
    if len(blocks) > 1:
        key_pos = jnp.zeros((1, span), jnp.int32)
        for n, flip in enumerate(offsets):
            start = jnp.bitwise_xor(seq_at, flip) * block_len
            key_pos = jnp.where(lane // block_len == n, lane - n * block_len + start, key_pos)
    rows = []
    for i in range(samples):
        column = jnp.maximum(own_slot_column(slots[i : i + 1, :], seq_at, cap), 0)
        reach = jnp.concatenate([column] * group, axis=0)
        allowed = key_pos <= reach
        pieces = []
        for g in range(kv_heads):
            left, right = g * HD, kv_width // 2 + g * HD
            keys = jnp.concatenate([b[i, :, left : left + HD] for b in blocks], axis=0)
            values = jnp.concatenate([b[i, :, right : right + HD] for b in blocks], axis=0)
            query = queries[i, g * group * cap : (g + 1) * group * cap, :]
            scores = lax.dot_general(
                query, keys, (((1,), (1,)), ((), ())), preferred_element_type=F32
            ) * HD ** (-0.5)
            scores = jnp.where(allowed, scores, FLOOR)
            top = jnp.max(scores, axis=1, keepdims=True)
            weights = jnp.where(allowed, jnp.exp(scores - top), 0.0)
            total = jnp.sum(weights, axis=1, keepdims=True)
            mixed = jnp.dot(weights.astype(BF16), values, preferred_element_type=F32)
            mixed = (mixed / total).astype(BF16)
            pieces += [mixed[h * cap : (h + 1) * cap, :] for h in range(group)]
        rows.append(jnp.concatenate(pieces, axis=1))
    attended = jnp.concatenate(rows, axis=0)
    out[...] = jnp.dot(attended, weight[...], preferred_element_type=F32).astype(BF16)


def norm_kernel(mine, other, residual, gain, full, half):
    hidden = residual[...].astype(F32) + (mine[...].astype(F32) + other[...].astype(F32))
    power = jnp.mean(hidden * hidden, axis=-1, keepdims=True)
    full[...] = (hidden * lax.rsqrt(power + 1e-06) * gain[...]).astype(BF16)
    if half is not None:
        count = half.shape[0]
        start = pl.multiple_of(lax.axis_index("vocab") * count, count)
        half[...] = full[pl.ds(start, count), :]


def fold(logits, wanted, first_row, top_ref, sum_ref, pick_ref):
    count, width = logits.shape
    tiles = logits.reshape(count // 8, 8, width)
    old = top_ref[...]
    new = jnp.maximum(old, jnp.max(tiles, axis=0))
    grown = jnp.sum(jnp.exp(tiles - new[None]), axis=0)
    sum_ref[...] = sum_ref[...] * jnp.exp(old - new) + grown
    top_ref[...] = new
    rows = iota(tiles.shape, 0) * 8 + iota(tiles.shape, 1)
    hit = rows == (wanted - first_row)[None]
    pick_ref[...] += jnp.sum(jnp.where(hit, tiles, 0.0), axis=0)


def score_tile(head, states, wanted, buffers, top_ref, sum_ref, pick_ref, step, unroll, base):
    top_ref[...] = jnp.full(top_ref.shape, FLOOR, F32)
    sum_ref[...] = jnp.zeros(sum_ref.shape, F32)
    pick_ref[...] = jnp.zeros(pick_ref.shape, F32)
    buffers[1][...] = jnp.full(buffers[1].shape, FLOOR, F32)
    local = wanted - base
    local = jnp.where((local >= 0) & (local < head.shape[0]), local, -(1 << 30))
    local = jnp.broadcast_to(local, top_ref.shape)

    def body(at, carry):
        for j in range(unroll):
            first = at * (unroll * step) + j * step
            block = head[pl.ds(pl.multiple_of(first, step), step), :]
            logits = lax.dot_general(
                block, states[...], (((1,), (1,)), ((), ())), preferred_element_type=F32
            )
            fold(buffers[(j + 1) % 2][...], local, first - step, top_ref, sum_ref, pick_ref)
            buffers[j % 2][...] = logits
        return carry

    total = head.shape[0]
    lax.fori_loop(0, total // (unroll * step), body, 0)
    fold(buffers[(unroll - 1) % 2][...], local, total - step, top_ref, sum_ref, pick_ref)
    top = jnp.max(top_ref[...], axis=0, keepdims=True)
    scale = jnp.exp(top_ref[...] - top)
    total = jnp.sum(sum_ref[...] * scale, axis=0, keepdims=True)
    return top + jnp.log(total), jnp.sum(pick_ref[...], axis=0, keepdims=True)


def vocab_base(shard_rows):
    owner = lax.axis_index("seq") * lax.axis_size("sample") + lax.axis_index("sample")
    return (owner * lax.axis_size("vocab") + lax.axis_index("vocab")) * shard_rows


def steps_of(shard_rows):
    for step in (256, 128, 64, 32, 16, 8):
        if shard_rows % (2 * step) == 0:
            unroll = 10 if shard_rows % (10 * step) == 0 else 2
            return step, unroll
    raise ValueError("head rows")


def column_kernel(places, step, unroll, last, head, meta, other_meta, *refs):
    before, refs = (refs[0], refs[1:]) if last is not None else (None, refs)
    inputs, refs = refs[: sum(place[2] for place in places)], refs[sum(place[2] for place in places) :]
    out, states, buf_a, buf_b, top_ref, sum_ref, pick_ref = refs[:7]
    rows = meta.shape[1]
    seq_at, core = lax.axis_index("seq"), lax.axis_index("vocab")
    wanted = []
    for n, place in enumerate(places):
        held = inputs[: place[2]]
        inputs = inputs[place[2] :]
        for part, ref in enumerate(held):
            count = ref.shape[0]
            start = n * rows
            if len(held) > 1:
                start = pl.multiple_of(start + jnp.bitwise_xor(core, part) * count, count)
            states[pl.ds(start, count), :] = ref[...]
        source = other_meta if place[0] else meta
        wanted.append(source[pl.ds(chip_of(place, seq_at, core), 1), :])
    logs, picks = score_tile(
        head, states, jnp.concatenate(wanted, axis=1), (buf_a, buf_b), top_ref, sum_ref, pick_ref,
        step, unroll, vocab_base(head.shape[0]),
    )
    results = [
        jnp.concatenate([logs[:, n * rows : (n + 1) * rows], picks[:, n * rows : (n + 1) * rows]], axis=1)
        for n in range(len(places))
    ]
    if last is None:
        for n, result in enumerate(results):
            out[n : n + 1, :] = result
        return
    message = refs[7]
    results = [before[n : n + 1, :] for n in range(len(last))] + results
    for place, result in zip([*last, *places], results):
        column = jnp.bitwise_xor(lax.axis_index("sample"), place[0])
        message[pl.ds(column * lax.axis_size("seq") + chip_of(place, seq_at, core), 1), :] = result
    out[...] = jnp.broadcast_to(message[...][None], out.shape)


def chip_of(place, seq_at, core):
    flip = place[1]
    if isinstance(flip, tuple):
        flip = jnp.where(core == 0, flip[0], flip[1])
    return jnp.bitwise_xor(seq_at, flip)


def column_scores(head, meta, other_meta, places, blocks, last=None, before=None):
    step, unroll = steps_of(head.shape[0])
    rows = meta.shape[1]
    total = rows * len(places)
    peers = 1
    for axis in CELL:
        peers *= lax.axis_size(axis)
    chips = peers // lax.axis_size("vocab")
    shape = (len(places), 2 * rows) if last is None else (peers, chips, 2 * rows)
    extra = [] if last is None else [before]
    return call(
        functools.partial(column_kernel, places, step, unroll, last),
        jax.ShapeDtypeStruct(shape, F32),
        [head, meta, other_meta, *extra, *blocks],
        [vmem()] * (3 + len(extra) + len(blocks)),
        scratch=[pltpu.VMEM((total, head.shape[1]), BF16)]
        + [pltpu.VMEM((step, total), F32)] * 2
        + [pltpu.VMEM((8, total), F32)] * 3
        + [pltpu.VMEM((chips, 2 * rows), F32)],
        flops=2 * total * head.shape[0] * head.shape[1],
    )


def tile_kernel(step, unroll, head, states, wanted, out, buf_a, buf_b, top_ref, sum_ref, pick_ref):
    parts = score_tile(
        head, states, wanted[...], (buf_a, buf_b), top_ref, sum_ref, pick_ref,
        step, unroll, vocab_base(head.shape[0]),
    )
    out[...] = jnp.concatenate(parts, axis=0)


def tiled_scores(head, states, wanted):
    step, unroll = steps_of(head.shape[0])
    count, width = states.shape
    tile = next(n for n in (256, 128, count) if count % n == 0)
    return pl.pallas_call(
        functools.partial(tile_kernel, step, unroll),
        grid=(count // tile,),
        out_shape=jax.ShapeDtypeStruct((2, count), F32),
        in_specs=[
            pl.BlockSpec(head.shape, lambda i: (0, 0)),
            pl.BlockSpec((tile, width), lambda i: (i, 0)),
            pl.BlockSpec((1, tile), lambda i: (0, i)),
        ],
        out_specs=pl.BlockSpec((2, tile), lambda i: (0, i)),
        scratch_shapes=[pltpu.VMEM((step, tile), F32)] * 2 + [pltpu.VMEM((8, tile), F32)] * 3,
        compiler_params=pltpu.CompilerParams(
            dimension_semantics=("arbitrary",), vmem_limit_bytes=52 * 2**20
        ),
    )(head, states, wanted)


def close_kernel(relative, columns, length, stats, *refs):
    metas, (tokens_out, scores_out, advantages_out, objective_out, tokens) = refs[:-5], refs[-5:]
    samples, cap = tokens_out.shape
    rows = samples * cap
    chips = tokens.shape[0]
    blocks = chips // columns
    prompts = samples * columns
    where, seq_at = lax.axis_index("sample"), lax.axis_index("seq")
    metas = [ref[...] for ref in metas]
    if relative:
        metas = [jnp.where(where == k, metas[0], metas[1]) for k in range(columns)]
    top = stats[0]
    for s in range(1, stats.shape[0]):
        top = jnp.maximum(top, stats[s])
    total = jnp.exp(stats[0] - top)
    pick = stats[0]
    for s in range(1, stats.shape[0]):
        total += jnp.exp(stats[s] - top)
        pick += stats[s]
    logprob = pick[:, rows:] - (top + jnp.log(total))[:, :rows]
    wanted = jnp.concatenate([meta[:blocks] for meta in metas], axis=0)
    tokens[...] = jnp.where(wanted >= 0, logprob, 0.0)
    paid = [meta[blocks : blocks + 1, :].astype(F32) for meta in metas]
    reward_sum = functools.reduce(lambda a, b: a + b, [jnp.sum(row) for row in paid])
    lane = iota((1, rows), 1)
    objective = jnp.float32(0)
    for k in range(columns):
        summed = jnp.sum(tokens[k * blocks : (k + 1) * blocks, :], axis=0, keepdims=True)
        for i in range(samples):
            score = jnp.sum(summed[:, i * cap : (i + 1) * cap]) / length
            reward = jnp.sum(jnp.where(lane == i, paid[k], 0.0))
            advantage = reward - (reward_sum - reward) / (prompts - 1)
            objective += advantage * score

            @pl.when(where == k)
            def _(score=score, advantage=advantage, i=i):
                scores_out[i] = score
                advantages_out[i] = advantage

    objective_out[0] = -(objective / prompts)
    mine = tokens[pl.ds(where * blocks + seq_at, 1), :]
    for i in range(samples):
        tokens_out[i : i + 1, :] = mine[:, i * cap : (i + 1) * cap]


def close(stats, metas, relative, samples, cap, length):
    columns = lax.axis_size("sample")
    outs = (
        jax.ShapeDtypeStruct((samples, cap), F32),
        jax.ShapeDtypeStruct((samples,), F32),
        jax.ShapeDtypeStruct((samples,), F32),
        jax.ShapeDtypeStruct((1,), F32),
    )
    return call(
        functools.partial(close_kernel, relative, columns, length),
        outs,
        [stats, *metas],
        [vmem()] * (1 + len(metas)),
        out_specs=(vmem(), smem(), smem(), smem()),
        scratch=[pltpu.VMEM((stats.shape[1], samples * cap), F32)],
    )


def steps(
    queries, key_states, value_states, residual, out_weight, norm_gain,
    vocab_head, targets, scored_slots, lengths, rewards,
):
    samples, block, width = queries.shape
    model_width = out_weight.shape[1]
    seq_size, sample_size, vocab_size = (lax.axis_size(axis) for axis in CELL)
    cap = scored_slots.shape[1] // seq_size
    length = targets.shape[1]
    rows = samples * cap
    short = (seq_size, sample_size, vocab_size) == (4, 2, 2) and samples % 2 == 0

    def send(array, target):
        pairs = []
        for z in range(seq_size):
            for x in range(sample_size):
                for c in range(vocab_size):
                    to_z, to_x, to_c = target(z, x, c)
                    source = (z * sample_size + x) * vocab_size + c
                    pairs.append((source, (to_z * sample_size + to_x) * vocab_size + to_c))
        return lax.ppermute(array, CELL, pairs)

    def across(array):
        return send(array, lambda z, x, c: (z, x, c ^ 1))

    def beside(array):
        return send(array, lambda z, x, c: (z, x ^ 1, c))

    kv_shape = (samples, block, 2 * key_states.shape[2])
    pair = call(
        pack_kernel,
        jax.ShapeDtypeStruct(kv_shape, BF16),
        [keep(key_states), keep(value_states)],
        [hbm(), hbm()],
        scratch=[pltpu.SemaphoreType.DMA((2,))],
        limit=4,
    )
    if short:
        offsets = (0, 1, 3, 2)
        far = send(pair, lambda z, x, c: (z ^ 2, x, c))
        near = send(pair, lambda z, x, c: (z ^ 1, x, c))
        wrap = send(pair, lambda z, x, c: (z ^ 3, x, c))
        blocks = [pair, near, wrap, far]
    else:
        offsets = (0,)
        blocks = [lax.all_gather(pair, "seq", axis=1, tiled=True)]
    heads = width // HD
    count = 10 if vocab_head.shape[0] % 160 == 0 else 1
    gain = norm_gain.reshape(1, model_width)
    slots, picked, picked_resid, meta, weight, gain, head = call(
        functools.partial(prep_kernel, count),
        (
            jax.ShapeDtypeStruct(scored_slots.shape, jnp.int32),
            jax.ShapeDtypeStruct((samples, heads * cap, HD), BF16),
            jax.ShapeDtypeStruct((rows, model_width), BF16),
            jax.ShapeDtypeStruct((seq_size + 1, rows), jnp.int32),
            pltpu.VMEM(out_weight.shape, BF16),
            pltpu.VMEM(gain.shape, F32),
            pltpu.VMEM(vocab_head.shape, BF16),
        ),
        [
            keep(array)
            for array in (
                scored_slots, targets, lengths, rewards, queries, residual,
                out_weight, gain, vocab_head,
            )
        ],
        [hbm()] * 9,
        scratch=[
            pltpu.VMEM(targets.shape, jnp.int32),
            pltpu.SMEM(lengths.shape, jnp.int32),
            pltpu.SMEM(rewards.shape, jnp.int32),
            pltpu.VMEM(queries.shape, BF16),
            pltpu.VMEM(residual.shape, BF16),
            pltpu.SemaphoreType.DMA((8 + count,)),
        ],
        limit=12,
    )
    head = pltpu.with_memory_space_constraint(head, pltpu.VMEM)
    weight = pltpu.with_memory_space_constraint(weight, pltpu.VMEM)
    partial_value = call(
        functools.partial(attend_kernel, offsets),
        jax.ShapeDtypeStruct((rows, model_width), BF16),
        [slots, picked, weight, *blocks],
        [vmem()] * (3 + len(blocks)),
    )
    if short:
        other_meta = beside(meta)
        other_partial = across(partial_value)
        normed, half = call(
            norm_kernel,
            (
                jax.ShapeDtypeStruct((rows, model_width), BF16),
                jax.ShapeDtypeStruct((rows // 2, model_width), BF16),
            ),
            [partial_value, other_partial, picked_resid, gain],
            [vmem()] * 4,
        )
        split = send(normed, lambda z, x, c: (z ^ (1, 3)[c], x, c))
        side = beside(half)
        far = send(half, lambda z, x, c: (z ^ 2, x, c))
        split_side = beside(split)
        side_far = send(side, lambda z, x, c: (z ^ 2, x, c))
        split_other = across(split)
        side_other = across(side)
        far_other = across(far)
        split_side_other = across(split_side)
        side_far_other = across(side_far)
        near = [(0, 0, 1), (0, (1, 3), 1), (0, (3, 1), 1), (1, 0, 2)]
        rest = [(0, 2, 2), (1, (1, 3), 1), (1, (3, 1), 1), (1, 2, 2)]
        first = column_scores(
            head, meta, other_meta, near, [normed, split, split_other, side, side_other]
        )
        stats = column_scores(
            head, meta, other_meta, rest,
            [far, far_other, split_side, split_side_other, side_far, side_far_other],
            last=near, before=first,
        )
        stats = lax.all_to_all(stats, CELL, 0, 0, tiled=True)
        return close(stats, [meta, other_meta], True, samples, cap, length)
    summed = lax.psum(partial_value, "vocab")
    normed = call(
        lambda a, b, r, g, out: norm_kernel(a, b, r, g, out, None),
        jax.ShapeDtypeStruct((rows, model_width), BF16),
        [summed, jnp.zeros_like(summed), picked_resid, gain],
        [vmem()] * 4,
    )
    every = lax.all_gather(normed, "seq", axis=0, tiled=True)
    every = lax.all_gather(every, "sample", axis=0, tiled=True)
    metas = lax.all_gather(meta, "sample", axis=0)
    logs, picks = tiled_scores(head, every, metas[:, :seq_size].reshape(1, -1))
    top = lax.pmax(logs, CELL)
    total, pick = lax.psum((jnp.exp(logs - top), picks), CELL)
    logs = (top + jnp.log(total)).reshape(1, -1, rows)
    stats = jnp.concatenate([logs, pick.reshape(1, -1, rows)], axis=2)
    metas = [metas[k] for k in range(sample_size)]
    return close(stats, metas, False, samples, cap, length)


def solution(mesh):
    in_specs = (
        P(("groups", "sample"), "seq", "vocab"),
        P(("groups", "sample"), "seq", "vocab"),
        P(("groups", "sample"), "seq", "vocab"),
        P(("groups", "sample"), "seq", None),
        P("vocab", None),
        P(),
        P(("seq", "sample", "vocab"), None),
        P(("groups", "sample"), None),
        P(("groups", "sample"), None),
        P(("groups", "sample")),
        P(("groups", "sample")),
    )
    out_specs = (
        P(("groups", "sample"), "seq"),
        P(("groups", "sample")),
        P(("groups", "sample")),
        P("groups"),
    )
    step = jax.shard_map(steps, mesh=mesh, in_specs=in_specs, out_specs=out_specs, check_vma=False)
    if tuple(mesh.shape[axis] for axis in CELL) != (4, 2, 2):
        return step
    return step
```

profile of v0, /device:TPU:0, one launch (start us, length us, event | category | flops | bytes accessed | tf_op | source)
XLA Modules:
  0.0 68.5 jit_solution(5058823417548487972)
XLA Ops:
  0.6 0.9 %shard_map.139.refs_0_ = bf16[4,64,256]{2,1,0:T(8,128)(2,1)S(1)} custom-call(bf16[4,64,128]{2,1,0:T(8,128)(2,1)} %keys.1, bf16[4,64,128]{2,1,0:T(8,128)(2,1)} %values.1), custom_call_target="tpu_custom_call" | custom-call | tf_op jit(solution)/shard_map/pallas_call | solution.py:38
  1.5 4.1 %collective-permute-start.3 = (bf16[4,64,256]{2,1,0:T(8,128)(2,1)S(1)}, bf16[4,64,256]{2,1,0:T(8,128)(2,1)S(1)}, u32[]{:S(2)}, u32[]{:S(2)}) collective-permute-start(bf16[4,64,256]{2,1,0:T(8,128)(2,1)S(1)} %shard_map.139.refs_0_), channel_id=1, source_target_pairs={{0,8},{1,9},{2,10},{3,11},{4,12},{5,13},{6,14},{7,15},{8,0},{9,1},... | collective-permute-start | bytes 393224 | tf_op jit(solution)/shard_map/ppermute | solution.py:412
  5.7 1.3 %collective-permute-start.2 = (bf16[4,64,256]{2,1,0:T(8,128)(2,1)S(1)}, bf16[4,64,256]{2,1,0:T(8,128)(2,1)S(1)}, u32[]{:S(2)}, u32[]{:S(2)}) collective-permute-start(bf16[4,64,256]{2,1,0:T(8,128)(2,1)S(1)} %shard_map.139.refs_0_), channel_id=1, source_target_pairs={{0,12},{1,13},{2,14},{3,15},{4,8},{5,9},{6,10},{7,11},{8,4},{9,5},... | collective-permute-start | bytes 393224 | tf_op jit(solution)/shard_map/ppermute | solution.py:412
  7.0 0.2 collective-permute-start.1
  7.2 1.3 %reshape.11.gain = f32[1,1792]{1,0:T(1,128)} reshape(f32[1792]{0:T(1024)} %param.16) | data formatting | bytes 14336 | tf_op jit(solution)/shard_map/reshape | solution.py:440
  8.5 7.8 %shard_map.138 = (s32[4,64]{1,0:T(4,128)S(1)}, bf16[4,112,128]{2,1,0:T(8,128)(2,1)S(1)}, bf16[64,1792]{1,0:T(8,128)(2,1)S(1)}, s32[5,64]{1,0:T(8,128)S(1)}, bf16...) custom-call(s32[4,64]{1,0:T(4,128)} %slots_in.1, s32[4,256]{1,0:T(4,128)} %targets_in.1, ...), custom_call_target="tpu_custom_call" | custom-call | tf_op jit(solution)/shard_map/pallas_call | solution.py:38
  16.3 0.0 collective-permute-done.3.refs_3_
  16.4 0.0 collective-permute-done.2.refs_2_
  16.4 0.0 collective-permute-done.1.refs_1_
  16.4 1.4 %shard_map.140.mine = bf16[64,1792]{1,0:T(8,128)(2,1)S(1)} custom-call(s32[4,64]{1,0:T(4,128)S(1)} %get-tuple-element.15.slots, bf16[4,112,128]{2,1,0:T(8,128)(2,1)S(1)} %get-tuple-element.16.queries, bf16[896,1792]{1,0:T(8,128)(2,1)S(1)} %get-tuple-element.17.weight, bf16[4,64,256]{2,1,0:T(8,128)(2,1)S(1)} %shard_map.139.refs_0_, ...), custom_call_target="tpu_custom_call" | custom-call | tf_op jit(solution)/shard_map/pallas_call | solution.py:38
  17.8 0.1 collective-permute-start.4
  17.9 1.5 %collective-permute-done.4.other = bf16[64,1792]{1,0:T(8,128)(2,1)S(1)} collective-permute-done((bf16[64,1792]{1,0:T(8,128)(2,1)S(1)}, bf16[64,1792]{1,0:T(8,128)(2,1)S(1)}, u32[]{:S(2)}, u32[]{:S(2)}) %collective-permute-start.4) | collective-permute-done | bytes 229408 | tf_op jit(solution)/shard_map/ppermute | solution.py:412
  19.3 0.2 shard_map.141
  19.6 2.0 %collective-permute-start.5 = (bf16[64,1792]{1,0:T(8,128)(2,1)S(1)}, bf16[64,1792]{1,0:T(8,128)(2,1)S(1)}, u32[]{:S(2)}, u32[]{:S(2)}) collective-permute-start(bf16[64,1792]{1,0:T(8,128)(2,1)S(1)} %get-tuple-element.20.refs_0_), channel_id=1, source_target_pairs={{0,4},{1,13},{2,6},{3,15},{4,0},{5,9},{6,2},{7,11},{8,12},{9,5},{1... | collective-permute-start | bytes 688136 | tf_op jit(solution)/shard_map/ppermute | solution.py:412
  21.6 1.5 %collective-permute-start.7 = (bf16[32,1792]{1,0:T(8,128)(2,1)S(1)}, bf16[32,1792]{1,0:T(8,128)(2,1)S(1)}, u32[]{:S(2)}, u32[]{:S(2)}) collective-permute-start(bf16[32,1792]{1,0:T(8,128)(2,1)S(1)} %get-tuple-element.21), channel_id=1, source_target_pairs={{0,2},{1,3},{2,0},{3,1},{4,6},{5,7},{6,4},{7,5},{8,10},{9,11},{10,... | collective-permute-start | bytes 344072 | tf_op jit(solution)/shard_map/ppermute | solution.py:412
  23.1 5.0 %collective-permute-done.5.refs_1_ = bf16[64,1792]{1,0:T(8,128)(2,1)S(1)} collective-permute-done((bf16[64,1792]{1,0:T(8,128)(2,1)S(1)}, bf16[64,1792]{1,0:T(8,128)(2,1)S(1)}, u32[]{:S(2)}, u32[]{:S(2)}) %collective-permute-start.5) | collective-permute-done | bytes 229408 | tf_op jit(solution)/shard_map/ppermute | solution.py:412
  28.1 1.5 %collective-permute-start.11 = (bf16[64,1792]{1,0:T(8,128)(2,1)S(1)}, bf16[64,1792]{1,0:T(8,128)(2,1)S(1)}, u32[]{:S(2)}, u32[]{:S(2)}) collective-permute-start(bf16[64,1792]{1,0:T(8,128)(2,1)S(1)} %collective-permute-done.5.refs_1_), channel_id=1, source_target_pairs={{0,2},{1,3},{2,0},{3,1},{4,6},{5,7},{6,4},{7,5},{8,10},{9,11},{10,... | collective-permute-start | bytes 688136 | tf_op jit(solution)/shard_map/ppermute | solution.py:412
  29.6 0.0 collective-permute-start.6
  29.6 0.5 collective-permute-start
  30.1 2.6 %collective-permute-start.9 = (bf16[32,1792]{1,0:T(8,128)(2,1)S(1)}, bf16[32,1792]{1,0:T(8,128)(2,1)S(1)}, u32[]{:S(2)}, u32[]{:S(2)}) collective-permute-start(bf16[32,1792]{1,0:T(8,128)(2,1)S(1)} %get-tuple-element.21), channel_id=1, source_target_pairs={{0,8},{1,9},{2,10},{3,11},{4,12},{5,13},{6,14},{7,15},{8,0},{9,1},... | collective-permute-start | bytes 344072 | tf_op jit(solution)/shard_map/ppermute | solution.py:412
  32.7 0.0 collective-permute-done.7.refs_3_
  32.7 0.3 collective-permute-start.13
  33.1 2.2 %collective-permute-done.other_meta.refs_1_ = s32[5,64]{1,0:T(8,128)S(1)} collective-permute-done((s32[5,64]{1,0:T(8,128)S(1)}, s32[5,64]{1,0:T(8,128)S(1)}, u32[]{:S(2)}, u32[]{:S(2)}) %collective-permute-start) | collective-permute-done | bytes 1312 | tf_op jit(solution)/shard_map/ppermute | solution.py:412
  35.3 0.0 collective-permute-start.8
  35.3 6.7 %collective-permute-done.9.refs_1_ = bf16[32,1792]{1,0:T(8,128)(2,1)S(1)} collective-permute-done((bf16[32,1792]{1,0:T(8,128)(2,1)S(1)}, bf16[32,1792]{1,0:T(8,128)(2,1)S(1)}, u32[]{:S(2)}, u32[]{:S(2)}) %collective-permute-start.9) | collective-permute-done | bytes 114720 | tf_op jit(solution)/shard_map/ppermute | solution.py:412
  42.0 0.0 collective-permute-start.10
  42.0 1.7 %collective-permute-done.13.refs_5_ = bf16[32,1792]{1,0:T(8,128)(2,1)S(1)} collective-permute-done((bf16[32,1792]{1,0:T(8,128)(2,1)S(1)}, bf16[32,1792]{1,0:T(8,128)(2,1)S(1)}, u32[]{:S(2)}, u32[]{:S(2)}) %collective-permute-start.13) | collective-permute-done | bytes 114720 | tf_op jit(solution)/shard_map/ppermute | solution.py:412
  43.7 0.0 collective-permute-start.14
  43.7 0.0 collective-permute-done.11.refs_3_
  43.7 0.5 collective-permute-start.12
  44.2 0.0 collective-permute-done.8.refs_4_
  44.2 0.0 collective-permute-done.6.refs_2_
  44.2 5.7 %shard_map.142.refs_0_ = f32[4,128]{1,0:T(4,128)S(1)} custom-call(bf16[5120,1792]{1,0:T(8,128)(2,1)S(1)} %get-tuple-element.13.head, s32[5,64]{1,0:T(8,128)S(1)} %get-tuple-element.14.meta.refs_0_, s32[5,64]{1,0:T(8,128)S(1)} %collective-permute-done.other_meta.refs_1_, bf16[64,1792]{1,0:T(8,128)(2,1)S(1)} %get-tuple-element.20.refs_0_, ...), custom_call_target="tpu_custom_call" | custom-call | flops 4697620480 | tf_op jit(solution)/shard_map/pallas_call | solution.py:38
  49.9 0.0 collective-permute-done.10.refs_2_
  49.9 0.0 collective-permute-done.14.refs_6_
  49.9 0.0 collective-permute-done.12.refs_4_
  49.9 5.7 %shard_map.143 = f32[16,8,128]{2,1,0:T(8,128)S(1)} custom-call(bf16[5120,1792]{1,0:T(8,128)(2,1)S(1)} %get-tuple-element.13.head, s32[5,64]{1,0:T(8,128)S(1)} %get-tuple-element.14.meta.refs_0_, s32[5,64]{1,0:T(8,128)S(1)} %collective-permute-done.other_meta.refs_1_, f32[4,128]{1,0:T(4,128)S(1)} %shard_map.142.refs_0_, ...), custom_call_target="tpu_custom_call" | custom-call | flops 4697620480 | tf_op jit(solution)/shard_map/pallas_call | solution.py:38
  55.6 11.9 %all_to_all.5.stats = f32[16,8,128]{2,1,0:T(8,128)S(1)} all-to-all(f32[16,8,128]{2,1,0:T(8,128)S(1)} %shard_map.143), channel_id=1, replica_groups=mesh['groups'=2,'seq'=4,'sample'=2,'vocab'=2] {'seq','sample','vocab'}, dimensions={0} | all-to-all | bytes 131072 | tf_op jit(solution)/shard_map/all_to_all | solution.py:510
  67.5 1.0 %shard_map.144 = (f32[4,16]{1,0:T(4,128)}, f32[4]{0:T(128)}, f32[4]{0:T(128)}, f32[1]{0:T(128)}) custom-call(f32[16,8,128]{2,1,0:T(8,128)S(1)} %all_to_all.5.stats, s32[5,64]{1,0:T(8,128)S(1)} %get-tuple-element.14.meta.refs_0_, s32[5,64]{1,0:T(8,128)S(1)} %collective-permute-done.other_meta.refs_1_), custom_call_target="tpu_custom_call" | custom-call | tf_op jit(solution)/shard_map/pallas_call | solution.py:38
Async XLA Ops:
  1.5 14.8 %collective-permute-start.3 = (bf16[4,64,256]{2,1,0:T(8,128)(2,1)S(1)}, bf16[4,64,256]{2,1,0:T(8,128)(2,1)S(1)}, u32[]{:S(2)}, u32[]{:S(2)}) collective-permute-start(bf16[4,64,256]{2,1,0:T(8,128)(2,1)S(1)} %shard_map.139.refs_0_), channel_id=1, source_target_pairs={{0,8},{1,9},{2,10},{3,11},{4,12},{5,13},{6,14},{7,15},{8,0},{9,1},... | collective-permute-start | bytes 393224 | tf_op jit(solution)/shard_map/ppermute | solution.py:412
  5.7 10.7 %collective-permute-start.2 = (bf16[4,64,256]{2,1,0:T(8,128)(2,1)S(1)}, bf16[4,64,256]{2,1,0:T(8,128)(2,1)S(1)}, u32[]{:S(2)}, u32[]{:S(2)}) collective-permute-start(bf16[4,64,256]{2,1,0:T(8,128)(2,1)S(1)} %shard_map.139.refs_0_), channel_id=1, source_target_pairs={{0,12},{1,13},{2,14},{3,15},{4,8},{5,9},{6,10},{7,11},{8,4},{9,5},... | collective-permute-start | bytes 393224 | tf_op jit(solution)/shard_map/ppermute | solution.py:412
  7.0 9.4 %collective-permute-start.1 = (bf16[4,64,256]{2,1,0:T(8,128)(2,1)S(1)}, bf16[4,64,256]{2,1,0:T(8,128)(2,1)S(1)}, u32[]{:S(2)}, u32[]{:S(2)}) collective-permute-start(bf16[4,64,256]{2,1,0:T(8,128)(2,1)S(1)} %shard_map.139.refs_0_), channel_id=1, source_target_pairs={{0,4},{1,5},{2,6},{3,7},{4,0},{5,1},{6,2},{7,3},{8,12},{9,13},{10,... | collective-permute-start | bytes 393224 | tf_op jit(solution)/shard_map/ppermute | solution.py:412
  17.8 1.6 %collective-permute-start.4 = (bf16[64,1792]{1,0:T(8,128)(2,1)S(1)}, bf16[64,1792]{1,0:T(8,128)(2,1)S(1)}, u32[]{:S(2)}, u32[]{:S(2)}) collective-permute-start(bf16[64,1792]{1,0:T(8,128)(2,1)S(1)} %shard_map.140.mine), channel_id=1, source_target_pairs={{0,1},{1,0},{2,3},{3,2},{4,5},{5,4},{6,7},{7,6},{8,9},{9,8},{10,11... | collective-permute-start | bytes 688136 | tf_op jit(solution)/shard_map/ppermute | solution.py:412
  19.6 8.5 %collective-permute-start.5 = (bf16[64,1792]{1,0:T(8,128)(2,1)S(1)}, bf16[64,1792]{1,0:T(8,128)(2,1)S(1)}, u32[]{:S(2)}, u32[]{:S(2)}) collective-permute-start(bf16[64,1792]{1,0:T(8,128)(2,1)S(1)} %get-tuple-element.20.refs_0_), channel_id=1, source_target_pairs={{0,4},{1,13},{2,6},{3,15},{4,0},{5,9},{6,2},{7,11},{8,12},{9,5},{1... | collective-permute-start | bytes 688136 | tf_op jit(solution)/shard_map/ppermute | solution.py:412
  21.6 11.1 %collective-permute-start.7 = (bf16[32,1792]{1,0:T(8,128)(2,1)S(1)}, bf16[32,1792]{1,0:T(8,128)(2,1)S(1)}, u32[]{:S(2)}, u32[]{:S(2)}) collective-permute-start(bf16[32,1792]{1,0:T(8,128)(2,1)S(1)} %get-tuple-element.21), channel_id=1, source_target_pairs={{0,2},{1,3},{2,0},{3,1},{4,6},{5,7},{6,4},{7,5},{8,10},{9,11},{10,... | collective-permute-start | bytes 344072 | tf_op jit(solution)/shard_map/ppermute | solution.py:412
  28.1 15.6 %collective-permute-start.11 = (bf16[64,1792]{1,0:T(8,128)(2,1)S(1)}, bf16[64,1792]{1,0:T(8,128)(2,1)S(1)}, u32[]{:S(2)}, u32[]{:S(2)}) collective-permute-start(bf16[64,1792]{1,0:T(8,128)(2,1)S(1)} %collective-permute-done.5.refs_1_), channel_id=1, source_target_pairs={{0,2},{1,3},{2,0},{3,1},{4,6},{5,7},{6,4},{7,5},{8,10},{9,11},{10,... | collective-permute-start | bytes 688136 | tf_op jit(solution)/shard_map/ppermute | solution.py:412
  29.6 14.6 %collective-permute-start.6 = (bf16[64,1792]{1,0:T(8,128)(2,1)S(1)}, bf16[64,1792]{1,0:T(8,128)(2,1)S(1)}, u32[]{:S(2)}, u32[]{:S(2)}) collective-permute-start(bf16[64,1792]{1,0:T(8,128)(2,1)S(1)} %collective-permute-done.5.refs_1_), channel_id=1, source_target_pairs={{0,1},{1,0},{2,3},{3,2},{4,5},{5,4},{6,7},{7,6},{8,9},{9,8},{10,11... | collective-permute-start | bytes 688136 | tf_op jit(solution)/shard_map/ppermute | solution.py:412
  29.6 5.7 %collective-permute-start = (s32[5,64]{1,0:T(8,128)S(1)}, s32[5,64]{1,0:T(8,128)S(1)}, u32[]{:S(2)}, u32[]{:S(2)}) collective-permute-start(s32[5,64]{1,0:T(8,128)S(1)} %get-tuple-element.14.meta.refs_0_), channel_id=1, source_target_pairs={{0,2},{1,3},{2,0},{3,1},{4,6},{5,7},{6,4},{7,5},{8,10},{9,11},{10,... | collective-permute-start | bytes 3848 | tf_op jit(solution)/shard_map/ppermute | solution.py:412
  30.1 11.8 %collective-permute-start.9 = (bf16[32,1792]{1,0:T(8,128)(2,1)S(1)}, bf16[32,1792]{1,0:T(8,128)(2,1)S(1)}, u32[]{:S(2)}, u32[]{:S(2)}) collective-permute-start(bf16[32,1792]{1,0:T(8,128)(2,1)S(1)} %get-tuple-element.21), channel_id=1, source_target_pairs={{0,8},{1,9},{2,10},{3,11},{4,12},{5,13},{6,14},{7,15},{8,0},{9,1},... | collective-permute-start | bytes 344072 | tf_op jit(solution)/shard_map/ppermute | solution.py:412
  32.7 11.0 %collective-permute-start.13 = (bf16[32,1792]{1,0:T(8,128)(2,1)S(1)}, bf16[32,1792]{1,0:T(8,128)(2,1)S(1)}, u32[]{:S(2)}, u32[]{:S(2)}) collective-permute-start(bf16[32,1792]{1,0:T(8,128)(2,1)S(1)} %collective-permute-done.7.refs_3_), channel_id=1, source_target_pairs={{0,8},{1,9},{2,10},{3,11},{4,12},{5,13},{6,14},{7,15},{8,0},{9,1},... | collective-permute-start | bytes 344072 | tf_op jit(solution)/shard_map/ppermute | solution.py:412
  35.3 8.9 %collective-permute-start.8 = (bf16[32,1792]{1,0:T(8,128)(2,1)S(1)}, bf16[32,1792]{1,0:T(8,128)(2,1)S(1)}, u32[]{:S(2)}, u32[]{:S(2)}) collective-permute-start(bf16[32,1792]{1,0:T(8,128)(2,1)S(1)} %collective-permute-done.7.refs_3_), channel_id=1, source_target_pairs={{0,1},{1,0},{2,3},{3,2},{4,5},{5,4},{6,7},{7,6},{8,9},{9,8},{10,11... | collective-permute-start | bytes 344072 | tf_op jit(solution)/shard_map/ppermute | solution.py:412
  42.0 7.9 %collective-permute-start.10 = (bf16[32,1792]{1,0:T(8,128)(2,1)S(1)}, bf16[32,1792]{1,0:T(8,128)(2,1)S(1)}, u32[]{:S(2)}, u32[]{:S(2)}) collective-permute-start(bf16[32,1792]{1,0:T(8,128)(2,1)S(1)} %collective-permute-done.9.refs_1_), channel_id=1, source_target_pairs={{0,1},{1,0},{2,3},{3,2},{4,5},{5,4},{6,7},{7,6},{8,9},{9,8},{10,11... | collective-permute-start | bytes 344072 | tf_op jit(solution)/shard_map/ppermute | solution.py:412
  43.7 6.2 %collective-permute-start.14 = (bf16[32,1792]{1,0:T(8,128)(2,1)S(1)}, bf16[32,1792]{1,0:T(8,128)(2,1)S(1)}, u32[]{:S(2)}, u32[]{:S(2)}) collective-permute-start(bf16[32,1792]{1,0:T(8,128)(2,1)S(1)} %collective-permute-done.13.refs_5_), channel_id=1, source_target_pairs={{0,1},{1,0},{2,3},{3,2},{4,5},{5,4},{6,7},{7,6},{8,9},{9,8},{10,11... | collective-permute-start | bytes 344072 | tf_op jit(solution)/shard_map/ppermute | solution.py:412
  43.7 6.2 %collective-permute-start.12 = (bf16[64,1792]{1,0:T(8,128)(2,1)S(1)}, bf16[64,1792]{1,0:T(8,128)(2,1)S(1)}, u32[]{:S(2)}, u32[]{:S(2)}) collective-permute-start(bf16[64,1792]{1,0:T(8,128)(2,1)S(1)} %collective-permute-done.11.refs_3_), channel_id=1, source_target_pairs={{0,1},{1,0},{2,3},{3,2},{4,5},{5,4},{6,7},{7,6},{8,9},{9,8},{10,11... | collective-permute-start | bytes 688136 | tf_op jit(solution)/shard_map/ppermute | solution.py:412
where the time goes:
time: 68.8 us; the launch traced here: 68.5 us
  Pallas kernels  22.7 us (33%)
  waiting for transfers between devices  17.1 us (25%)
  starting transfers between devices  14.8 us (22%)
  blocking collectives  11.9 us (17%)
  local copies, waits for them, and re-layouts  1.3 us (2%)
  between operations  0.72 us (1%)
    pallas_call x7, Pallas kernels, call(): pl.pallas_call(body, cost_estimate=cost, out_shape=outs, in_specs=in_spec...  22.7 us
    ppermute x15, waiting for transfers between devices, send(): return lax.ppermute(array, CELL, pairs)  17.1 us
    ppermute x15, starting transfers between devices, send(): return lax.ppermute(array, CELL, pairs)  14.8 us
    all_to_all x1, blocking collectives, steps(): stats = lax.all_to_all(stats, CELL, 0, 0, tiled=True)  11.9 us
  transfers between devices with their start and end apart: 15, of which 5 were waited for; matrix products, arithmetic and copies ran while one was open for 2% of the time, Pallas kernels for 20%

commit v1 on v0

--- a/solution.py
+++ b/solution.py
@@ -82,7 +82,7 @@
     step = head.shape[0] // count
     moves = [
         (slots_in, slots), (targets_in, targets), (lengths_in, lengths), (rewards_in, rewards),
-        (queries, q_in), (residual, r_in), (weight, weight_out), (gain, gain_out),
+        (queries, q_in), (residual, r_in), (weight, weight_out), (gain, gain_out.at[0]),
     ]
     for n in range(count):
         moves.append((head.at[pl.ds(n * step, step), :], head_out.at[pl.ds(n * step, step), :]))
@@ -224,29 +224,38 @@
 def steps_of(shard_rows):
     for step in (256, 128, 64, 32, 16, 8):
         if shard_rows % (2 * step) == 0:
-            unroll = 10 if shard_rows % (10 * step) == 0 else 2
+            unroll = next(n for n in (20, 10, 4, 2) if shard_rows % (n * step) == 0)
             return step, unroll
     raise ValueError("head rows")
 
 
 def column_kernel(places, step, unroll, last, head, meta, other_meta, *refs):
     before, refs = (refs[0], refs[1:]) if last is not None else (None, refs)
-    inputs, refs = refs[: sum(place[2] for place in places)], refs[sum(place[2] for place in places) :]
+    count = sum(abs(place[2]) for place in places)
+    inputs, refs = refs[:count], refs[count:]
     out, states, buf_a, buf_b, top_ref, sum_ref, pick_ref = refs[:7]
     rows = meta.shape[1]
     seq_at, core = lax.axis_index("seq"), lax.axis_index("vocab")
     wanted = []
     for n, place in enumerate(places):
-        held = inputs[: place[2]]
-        inputs = inputs[place[2] :]
-        for part, ref in enumerate(held):
-            count = ref.shape[0]
-            start = n * rows
-            if len(held) > 1:
-                start = pl.multiple_of(start + jnp.bitwise_xor(core, part) * count, count)
-            states[pl.ds(start, count), :] = ref[...]
-        source = other_meta if place[0] else meta
-        wanted.append(source[pl.ds(chip_of(place, seq_at, core), 1), :])
+        held = inputs[: abs(place[2])]
+        inputs = inputs[abs(place[2]) :]
+        if place[2] < 0:
+            for part, ref in enumerate(held):
+
+                @pl.when(core == 1 - part)
+                def _(ref=ref, n=n):
+                    states[n * rows : (n + 1) * rows, :] = ref[...]
+        else:
+            for part, ref in enumerate(held):
+                count = ref.shape[0]
+                start = n * rows
+                if len(held) > 1:
+                    start = pl.multiple_of(start + jnp.bitwise_xor(core, part) * count, count)
+                states[pl.ds(start, count), :] = ref[...]
+        row = pl.ds(chip_of(place[1], seq_at, core), 1)
+        column = of_core(place[0], core)
+        wanted.append(jnp.where(column == 1, other_meta[row, :], meta[row, :]))
     logs, picks = score_tile(
         head, states, jnp.concatenate(wanted, axis=1), (buf_a, buf_b), top_ref, sum_ref, pick_ref,
         step, unroll, vocab_base(head.shape[0]),
@@ -262,16 +271,18 @@
     message = refs[7]
     results = [before[n : n + 1, :] for n in range(len(last))] + results
     for place, result in zip([*last, *places], results):
-        column = jnp.bitwise_xor(lax.axis_index("sample"), place[0])
-        message[pl.ds(column * lax.axis_size("seq") + chip_of(place, seq_at, core), 1), :] = result
+        column = jnp.bitwise_xor(lax.axis_index("sample"), of_core(place[0], core))
+        row = column * lax.axis_size("seq") + chip_of(place[1], seq_at, core)
+        message[pl.ds(row, 1), :] = result
     out[...] = jnp.broadcast_to(message[...][None], out.shape)
 
 
-def chip_of(place, seq_at, core):
-    flip = place[1]
-    if isinstance(flip, tuple):
-        flip = jnp.where(core == 0, flip[0], flip[1])
-    return jnp.bitwise_xor(seq_at, flip)
+def of_core(choice, core):
+    return jnp.where(core == 0, *choice) if isinstance(choice, tuple) else choice
+
+
+def chip_of(flip, seq_at, core):
+    return jnp.bitwise_xor(seq_at, of_core(flip, core))
 
 
 def column_scores(head, meta, other_meta, places, blocks, last=None, before=None):
@@ -399,17 +410,30 @@
     cap = scored_slots.shape[1] // seq_size
     length = targets.shape[1]
     rows = samples * cap
-    short = (seq_size, sample_size, vocab_size) == (4, 2, 2) and samples % 2 == 0
+    sizes = tuple(lax.axis_size(axis) for axis in ("groups",) + CELL)
+    short = sizes == (2, 4, 2, 2) and samples % 2 == 0
 
     def send(array, target):
         pairs = []
         for z in range(seq_size):
             for x in range(sample_size):
                 for c in range(vocab_size):
-                    to_z, to_x, to_c = target(z, x, c)
-                    source = (z * sample_size + x) * vocab_size + c
-                    pairs.append((source, (to_z * sample_size + to_x) * vocab_size + to_c))
+                    place = target(z, x, c)
+                    if place is not None:
+                        source = (z * sample_size + x) * vocab_size + c
+                        to = (place[0] * sample_size + place[1]) * vocab_size + place[2]
+                        pairs.append((source, to))
         return lax.ppermute(array, CELL, pairs)
+
+    def aside(array):
+        pairs = []
+        for g in range(2):
+            for z in range(seq_size):
+                for x in range(sample_size):
+                    at = ((g * seq_size + z) * sample_size + x) * vocab_size
+                    pairs.append((at, (((1 - g) * seq_size + z) * sample_size + x) * vocab_size))
+                    pairs.append((at + 1, ((g * seq_size + z) * sample_size + 1 - x) * vocab_size + 1))
+        return lax.ppermute(array, ("groups",) + CELL, pairs)
 
     def across(array):
         return send(array, lambda z, x, c: (z, x, c ^ 1))
@@ -437,7 +461,6 @@
         blocks = [lax.all_gather(pair, "seq", axis=1, tiled=True)]
     heads = width // HD
     count = 10 if vocab_head.shape[0] % 160 == 0 else 1
-    gain = norm_gain.reshape(1, model_width)
     slots, picked, picked_resid, meta, weight, gain, head = call(
         functools.partial(prep_kernel, count),
         (
@@ -446,14 +469,14 @@
             jax.ShapeDtypeStruct((rows, model_width), BF16),
             jax.ShapeDtypeStruct((seq_size + 1, rows), jnp.int32),
             pltpu.VMEM(out_weight.shape, BF16),
-            pltpu.VMEM(gain.shape, F32),
+            pltpu.VMEM((1, model_width), F32),
             pltpu.VMEM(vocab_head.shape, BF16),
         ),
         [
             keep(array)
             for array in (
                 scored_slots, targets, lengths, rewards, queries, residual,
-                out_weight, gain, vocab_head,
+                out_weight, norm_gain, vocab_head,
             )
         ],
         [hbm()] * 9,
@@ -489,22 +512,22 @@
         )
         split = send(normed, lambda z, x, c: (z ^ (1, 3)[c], x, c))
         side = beside(half)
-        far = send(half, lambda z, x, c: (z ^ 2, x, c))
-        split_side = beside(split)
+        turn = send(split, lambda z, x, c: (z, x ^ 1, c) if c == 0 else (z ^ 1, x, c))
+        split_side = aside(split)
         side_far = send(side, lambda z, x, c: (z ^ 2, x, c))
         split_other = across(split)
         side_other = across(side)
-        far_other = across(far)
+        turn_other = across(turn)
         split_side_other = across(split_side)
         side_far_other = across(side_far)
         near = [(0, 0, 1), (0, (1, 3), 1), (0, (3, 1), 1), (1, 0, 2)]
-        rest = [(0, 2, 2), (1, (1, 3), 1), (1, (3, 1), 1), (1, 2, 2)]
+        rest = [((1, 0), (1, 2), 1), ((0, 1), (2, 1), 1), (1, 3, -2), (1, 2, 2)]
         first = column_scores(
             head, meta, other_meta, near, [normed, split, split_other, side, side_other]
         )
         stats = column_scores(
             head, meta, other_meta, rest,
-            [far, far_other, split_side, split_side_other, side_far, side_far_other],
+            [turn, turn_other, split_side, split_side_other, side_far, side_far_other],
             last=near, before=first,
         )
         stats = lax.all_to_all(stats, CELL, 0, 0, tiled=True)
@@ -549,6 +572,6 @@
         P("groups"),
     )
     step = jax.shard_map(steps, mesh=mesh, in_specs=in_specs, out_specs=out_specs, check_vma=False)
-    if tuple(mesh.shape[axis] for axis in CELL) != (4, 2, 2):
+    if tuple(mesh.shape[axis] for axis in ("groups",) + CELL) != (2, 4, 2, 2):
         return step
     return step

time: 68.8 us -> 64.8 us (0.942)
  waiting for transfers between devices: 17.1 us -> 14 us
  local copies, waits for them, and re-layouts: 1.3 us -> 0 us
  starting transfers between devices: 14.8 us -> 15.9 us
    ppermute x15 -> x14, waiting for transfers between devices: 17.1 us -> 14 us  [send(): return lax.ppermute(array, CELL, pairs)]
    ppermute x0 -> x1, starting transfers between devices: none -> 1.52 us  [aside(): return lax.ppermute(array, ('groups',) + CELL, pairs)]
    reshape x1 -> x0, local copies, waits for them, and re-layouts: 1.3 us -> none  [steps(): gain = norm_gain.reshape(1, model_width)]
    ppermute x15 -> x14, starting transfers between devices: 14.8 us -> 14.4 us  [send(): return lax.ppermute(array, CELL, pairs)]
  transfers between devices with their start and end apart: 15 -> 15, of which waited for: 5 -> 6; matrix products, arithmetic and copies ran while one was open for 2% -> 0% of each run, Pallas kernels for 20% -> 21%
where the time goes in v1:
time: 64.8 us; the launch traced here: 64.6 us
  Pallas kernels  22.5 us (35%)
  starting transfers between devices  15.9 us (25%)
  waiting for transfers between devices  14 us (22%)
  blocking collectives  11.5 us (18%)
  between operations  0.69 us (1%)
    pallas_call x7, Pallas kernels, call(): pl.pallas_call(body, cost_estimate=cost, out_shape=outs, in_specs=in_spec...  22.5 us
    ppermute x14, starting transfers between devices, send(): return lax.ppermute(array, CELL, pairs)  14.4 us
    ppermute x14, waiting for transfers between devices, send(): return lax.ppermute(array, CELL, pairs)  14 us
    all_to_all x1, blocking collectives, steps(): stats = lax.all_to_all(stats, CELL, 0, 0, tiled=True)  11.5 us
    ppermute x1, starting transfers between devices, aside(): return lax.ppermute(array, ('groups',) + CELL, pairs)  1.52 us
  transfers between devices with their start and end apart: 15, of which 6 were waited for; matrix products, arithmetic and copies ran while one was open for 0% of the time, Pallas kernels for 21%

profile of v1, /device:TPU:0, one launch (start us, length us, event | category | flops | bytes accessed | tf_op | source)
XLA Modules:
  0.0 64.6 jit_solution(3655792597917843761)
XLA Ops:
  0.6 0.9 %shard_map.139.refs_0_ = bf16[4,64,256]{2,1,0:T(8,128)(2,1)S(1)} custom-call(bf16[4,64,128]{2,1,0:T(8,128)(2,1)} %keys.1, bf16[4,64,128]{2,1,0:T(8,128)(2,1)} %values.1), custom_call_target="tpu_custom_call" | custom-call | tf_op jit(solution)/shard_map/pallas_call | solution.py:38
  1.5 4.1 %collective-permute-start.3 = (bf16[4,64,256]{2,1,0:T(8,128)(2,1)S(1)}, bf16[4,64,256]{2,1,0:T(8,128)(2,1)S(1)}, u32[]{:S(2)}, u32[]{:S(2)}) collective-permute-start(bf16[4,64,256]{2,1,0:T(8,128)(2,1)S(1)} %shard_map.139.refs_0_), channel_id=1, source_target_pairs={{0,8},{1,9},{2,10},{3,11},{4,12},{5,13},{6,14},{7,15},{8,0},{9,1},... | collective-permute-start | bytes 393224 | tf_op jit(solution)/shard_map/ppermute | solution.py:426
  5.7 1.3 %collective-permute-start.2 = (bf16[4,64,256]{2,1,0:T(8,128)(2,1)S(1)}, bf16[4,64,256]{2,1,0:T(8,128)(2,1)S(1)}, u32[]{:S(2)}, u32[]{:S(2)}) collective-permute-start(bf16[4,64,256]{2,1,0:T(8,128)(2,1)S(1)} %shard_map.139.refs_0_), channel_id=1, source_target_pairs={{0,12},{1,13},{2,14},{3,15},{4,8},{5,9},{6,10},{7,11},{8,4},{9,5},... | collective-permute-start | bytes 393224 | tf_op jit(solution)/shard_map/ppermute | solution.py:426
  7.0 0.2 collective-permute-start.1
  7.2 7.8 %shard_map.138 = (s32[4,64]{1,0:T(4,128)S(1)}, bf16[4,112,128]{2,1,0:T(8,128)(2,1)S(1)}, bf16[64,1792]{1,0:T(8,128)(2,1)S(1)}, s32[5,64]{1,0:T(8,128)S(1)}, bf16...) custom-call(s32[4,64]{1,0:T(4,128)} %slots_in.1, s32[4,256]{1,0:T(4,128)} %targets_in.1, ...), custom_call_target="tpu_custom_call" | custom-call | tf_op jit(solution)/shard_map/pallas_call | solution.py:38
  15.1 0.6 collective-permute-done.3.refs_3_
  15.7 0.0 collective-permute-done.2.refs_2_
  15.7 0.5 collective-permute-done.1.refs_1_
  16.2 1.4 %shard_map.140.mine = bf16[64,1792]{1,0:T(8,128)(2,1)S(1)} custom-call(s32[4,64]{1,0:T(4,128)S(1)} %get-tuple-element.15.slots, bf16[4,112,128]{2,1,0:T(8,128)(2,1)S(1)} %get-tuple-element.16.queries, bf16[896,1792]{1,0:T(8,128)(2,1)S(1)} %get-tuple-element.17.weight, bf16[4,64,256]{2,1,0:T(8,128)(2,1)S(1)} %shard_map.139.refs_0_, ...), custom_call_target="tpu_custom_call" | custom-call | tf_op jit(solution)/shard_map/pallas_call | solution.py:38
  17.6 0.1 collective-permute-start.4
  17.6 1.5 %collective-permute-done.4.other = bf16[64,1792]{1,0:T(8,128)(2,1)S(1)} collective-permute-done((bf16[64,1792]{1,0:T(8,128)(2,1)S(1)}, bf16[64,1792]{1,0:T(8,128)(2,1)S(1)}, u32[]{:S(2)}, u32[]{:S(2)}) %collective-permute-start.4) | collective-permute-done | bytes 229408 | tf_op jit(solution)/shard_map/ppermute | solution.py:426
  19.1 0.2 shard_map.141
  19.3 2.3 %collective-permute-start.5 = (bf16[64,1792]{1,0:T(8,128)(2,1)S(1)}, bf16[64,1792]{1,0:T(8,128)(2,1)S(1)}, u32[]{:S(2)}, u32[]{:S(2)}) collective-permute-start(bf16[64,1792]{1,0:T(8,128)(2,1)S(1)} %get-tuple-element.20.refs_0_), channel_id=1, source_target_pairs={{0,4},{1,13},{2,6},{3,15},{4,0},{5,9},{6,2},{7,11},{8,12},{9,5},{1... | collective-permute-start | bytes 688136 | tf_op jit(solution)/shard_map/ppermute | solution.py:426
  21.6 1.5 %collective-permute-start.7 = (bf16[32,1792]{1,0:T(8,128)(2,1)S(1)}, bf16[32,1792]{1,0:T(8,128)(2,1)S(1)}, u32[]{:S(2)}, u32[]{:S(2)}) collective-permute-start(bf16[32,1792]{1,0:T(8,128)(2,1)S(1)} %get-tuple-element.21), channel_id=1, source_target_pairs={{0,2},{1,3},{2,0},{3,1},{4,6},{5,7},{6,4},{7,5},{8,10},{9,11},{10,... | collective-permute-start | bytes 344072 | tf_op jit(solution)/shard_map/ppermute | solution.py:426
  23.1 5.0 %collective-permute-done.5.refs_1_ = bf16[64,1792]{1,0:T(8,128)(2,1)S(1)} collective-permute-done((bf16[64,1792]{1,0:T(8,128)(2,1)S(1)}, bf16[64,1792]{1,0:T(8,128)(2,1)S(1)}, u32[]{:S(2)}, u32[]{:S(2)}) %collective-permute-start.5) | collective-permute-done | bytes 229408 | tf_op jit(solution)/shard_map/ppermute | solution.py:426
  28.1 1.5 %collective-permute-start.11 = (bf16[64,1792]{1,0:T(8,128)(2,1)S(1)}, bf16[64,1792]{1,0:T(8,128)(2,1)S(1)}, u32[]{:S(2)}, u32[]{:S(2)}) collective-permute-start(bf16[64,1792]{1,0:T(8,128)(2,1)S(1)} %collective-permute-done.5.refs_1_), channel_id=1, source_target_pairs={{0,16},{1,3},{2,18},{3,1},{4,20},{5,7},{6,22},{7,5},{8,24},{9,11},... | collective-permute-start | bytes 688136 | tf_op jit(solution)/shard_map/ppermute | solution.py:436
  29.6 1.5 %collective-permute-start.9 = (bf16[64,1792]{1,0:T(8,128)(2,1)S(1)}, bf16[64,1792]{1,0:T(8,128)(2,1)S(1)}, u32[]{:S(2)}, u32[]{:S(2)}) collective-permute-start(bf16[64,1792]{1,0:T(8,128)(2,1)S(1)} %collective-permute-done.5.refs_1_), channel_id=1, source_target_pairs={{0,2},{1,5},{2,0},{3,7},{4,6},{5,1},{6,4},{7,3},{8,10},{9,13},{10,... | collective-permute-start | bytes 688136 | tf_op jit(solution)/shard_map/ppermute | solution.py:426
  31.1 0.0 collective-permute-start.6
  31.1 0.5 collective-permute-start
  31.6 0.0 collective-permute-done.7.refs_3_
  31.6 2.2 %collective-permute-start.13 = (bf16[32,1792]{1,0:T(8,128)(2,1)S(1)}, bf16[32,1792]{1,0:T(8,128)(2,1)S(1)}, u32[]{:S(2)}, u32[]{:S(2)}) collective-permute-start(bf16[32,1792]{1,0:T(8,128)(2,1)S(1)} %collective-permute-done.7.refs_3_), channel_id=1, source_target_pairs={{0,8},{1,9},{2,10},{3,11},{4,12},{5,13},{6,14},{7,15},{8,0},{9,1},... | collective-permute-start | bytes 344072 | tf_op jit(solution)/shard_map/ppermute | solution.py:426
  33.8 1.9 %collective-permute-done.other_meta.refs_1_ = s32[5,64]{1,0:T(8,128)S(1)} collective-permute-done((s32[5,64]{1,0:T(8,128)S(1)}, s32[5,64]{1,0:T(8,128)S(1)}, u32[]{:S(2)}, u32[]{:S(2)}) %collective-permute-start) | collective-permute-done | bytes 1312 | tf_op jit(solution)/shard_map/ppermute | solution.py:426
  35.7 0.0 collective-permute-start.8
  35.7 4.6 %collective-permute-done.13.refs_5_ = bf16[32,1792]{1,0:T(8,128)(2,1)S(1)} collective-permute-done((bf16[32,1792]{1,0:T(8,128)(2,1)S(1)}, bf16[32,1792]{1,0:T(8,128)(2,1)S(1)}, u32[]{:S(2)}, u32[]{:S(2)}) %collective-permute-start.13) | collective-permute-done | bytes 114720 | tf_op jit(solution)/shard_map/ppermute | solution.py:426
  40.2 0.0 collective-permute-start.14
  40.2 0.0 collective-permute-done.11.refs_3_
  40.2 0.5 collective-permute-start.12
  40.8 0.0 collective-permute-done.9.refs_1_
  40.8 0.1 collective-permute-start.10
  40.8 0.0 collective-permute-done.8.refs_4_
  40.8 0.0 collective-permute-done.6.refs_2_
  40.8 5.6 %shard_map.142.refs_0_ = f32[4,128]{1,0:T(4,128)S(1)} custom-call(bf16[5120,1792]{1,0:T(8,128)(2,1)S(1)} %get-tuple-element.13.head, s32[5,64]{1,0:T(8,128)S(1)} %get-tuple-element.14.meta.refs_0_, s32[5,64]{1,0:T(8,128)S(1)} %collective-permute-done.other_meta.refs_1_, bf16[64,1792]{1,0:T(8,128)(2,1)S(1)} %get-tuple-element.20.refs_0_, ...), custom_call_target="tpu_custom_call" | custom-call | flops 4697620480 | tf_op jit(solution)/shard_map/pallas_call | solution.py:38
  46.5 0.0 collective-permute-done.14.refs_6_
  46.5 0.0 collective-permute-done.12.refs_4_
  46.5 0.0 collective-permute-done.10.refs_2_
  46.5 5.6 %shard_map.143 = f32[16,8,128]{2,1,0:T(8,128)S(1)} custom-call(bf16[5120,1792]{1,0:T(8,128)(2,1)S(1)} %get-tuple-element.13.head, s32[5,64]{1,0:T(8,128)S(1)} %get-tuple-element.14.meta.refs_0_, s32[5,64]{1,0:T(8,128)S(1)} %collective-permute-done.other_meta.refs_1_, f32[4,128]{1,0:T(4,128)S(1)} %shard_map.142.refs_0_, ...), custom_call_target="tpu_custom_call" | custom-call | flops 4697620480 | tf_op jit(solution)/shard_map/pallas_call | solution.py:38
  52.1 11.5 %all_to_all.5.stats = f32[16,8,128]{2,1,0:T(8,128)S(1)} all-to-all(f32[16,8,128]{2,1,0:T(8,128)S(1)} %shard_map.143), channel_id=1, replica_groups=mesh['groups'=2,'seq'=4,'sample'=2,'vocab'=2] {'seq','sample','vocab'}, dimensions={0} | all-to-all | bytes 131072 | tf_op jit(solution)/shard_map/all_to_all | solution.py:533
  63.6 1.0 %shard_map.144 = (f32[4,16]{1,0:T(4,128)}, f32[4]{0:T(128)}, f32[4]{0:T(128)}, f32[1]{0:T(128)}) custom-call(f32[16,8,128]{2,1,0:T(8,128)S(1)} %all_to_all.5.stats, s32[5,64]{1,0:T(8,128)S(1)} %get-tuple-element.14.meta.refs_0_, s32[5,64]{1,0:T(8,128)S(1)} %collective-permute-done.other_meta.refs_1_), custom_call_target="tpu_custom_call" | custom-call | tf_op jit(solution)/shard_map/pallas_call | solution.py:38
Async XLA Ops:
  1.5 14.1 %collective-permute-start.3 = (bf16[4,64,256]{2,1,0:T(8,128)(2,1)S(1)}, bf16[4,64,256]{2,1,0:T(8,128)(2,1)S(1)}, u32[]{:S(2)}, u32[]{:S(2)}) collective-permute-start(bf16[4,64,256]{2,1,0:T(8,128)(2,1)S(1)} %shard_map.139.refs_0_), channel_id=1, source_target_pairs={{0,8},{1,9},{2,10},{3,11},{4,12},{5,13},{6,14},{7,15},{8,0},{9,1},... | collective-permute-start | bytes 393224 | tf_op jit(solution)/shard_map/ppermute | solution.py:426
  5.7 10.0 %collective-permute-start.2 = (bf16[4,64,256]{2,1,0:T(8,128)(2,1)S(1)}, bf16[4,64,256]{2,1,0:T(8,128)(2,1)S(1)}, u32[]{:S(2)}, u32[]{:S(2)}) collective-permute-start(bf16[4,64,256]{2,1,0:T(8,128)(2,1)S(1)} %shard_map.139.refs_0_), channel_id=1, source_target_pairs={{0,12},{1,13},{2,14},{3,15},{4,8},{5,9},{6,10},{7,11},{8,4},{9,5},... | collective-permute-start | bytes 393224 | tf_op jit(solution)/shard_map/ppermute | solution.py:426
  7.0 9.2 %collective-permute-start.1 = (bf16[4,64,256]{2,1,0:T(8,128)(2,1)S(1)}, bf16[4,64,256]{2,1,0:T(8,128)(2,1)S(1)}, u32[]{:S(2)}, u32[]{:S(2)}) collective-permute-start(bf16[4,64,256]{2,1,0:T(8,128)(2,1)S(1)} %shard_map.139.refs_0_), channel_id=1, source_target_pairs={{0,4},{1,5},{2,6},{3,7},{4,0},{5,1},{6,2},{7,3},{8,12},{9,13},{10,... | collective-permute-start | bytes 393224 | tf_op jit(solution)/shard_map/ppermute | solution.py:426
  17.6 1.6 %collective-permute-start.4 = (bf16[64,1792]{1,0:T(8,128)(2,1)S(1)}, bf16[64,1792]{1,0:T(8,128)(2,1)S(1)}, u32[]{:S(2)}, u32[]{:S(2)}) collective-permute-start(bf16[64,1792]{1,0:T(8,128)(2,1)S(1)} %shard_map.140.mine), channel_id=1, source_target_pairs={{0,1},{1,0},{2,3},{3,2},{4,5},{5,4},{6,7},{7,6},{8,9},{9,8},{10,11... | collective-permute-start | bytes 688136 | tf_op jit(solution)/shard_map/ppermute | solution.py:426
  19.3 8.7 %collective-permute-start.5 = (bf16[64,1792]{1,0:T(8,128)(2,1)S(1)}, bf16[64,1792]{1,0:T(8,128)(2,1)S(1)}, u32[]{:S(2)}, u32[]{:S(2)}) collective-permute-start(bf16[64,1792]{1,0:T(8,128)(2,1)S(1)} %get-tuple-element.20.refs_0_), channel_id=1, source_target_pairs={{0,4},{1,13},{2,6},{3,15},{4,0},{5,9},{6,2},{7,11},{8,12},{9,5},{1... | collective-permute-start | bytes 688136 | tf_op jit(solution)/shard_map/ppermute | solution.py:426
  21.6 10.0 %collective-permute-start.7 = (bf16[32,1792]{1,0:T(8,128)(2,1)S(1)}, bf16[32,1792]{1,0:T(8,128)(2,1)S(1)}, u32[]{:S(2)}, u32[]{:S(2)}) collective-permute-start(bf16[32,1792]{1,0:T(8,128)(2,1)S(1)} %get-tuple-element.21), channel_id=1, source_target_pairs={{0,2},{1,3},{2,0},{3,1},{4,6},{5,7},{6,4},{7,5},{8,10},{9,11},{10,... | collective-permute-start | bytes 344072 | tf_op jit(solution)/shard_map/ppermute | solution.py:426
  28.1 12.2 %collective-permute-start.11 = (bf16[64,1792]{1,0:T(8,128)(2,1)S(1)}, bf16[64,1792]{1,0:T(8,128)(2,1)S(1)}, u32[]{:S(2)}, u32[]{:S(2)}) collective-permute-start(bf16[64,1792]{1,0:T(8,128)(2,1)S(1)} %collective-permute-done.5.refs_1_), channel_id=1, source_target_pairs={{0,16},{1,3},{2,18},{3,1},{4,20},{5,7},{6,22},{7,5},{8,24},{9,11},... | collective-permute-start | bytes 688136 | tf_op jit(solution)/shard_map/ppermute | solution.py:436
  29.6 11.2 %collective-permute-start.9 = (bf16[64,1792]{1,0:T(8,128)(2,1)S(1)}, bf16[64,1792]{1,0:T(8,128)(2,1)S(1)}, u32[]{:S(2)}, u32[]{:S(2)}) collective-permute-start(bf16[64,1792]{1,0:T(8,128)(2,1)S(1)} %collective-permute-done.5.refs_1_), channel_id=1, source_target_pairs={{0,2},{1,5},{2,0},{3,7},{4,6},{5,1},{6,4},{7,3},{8,10},{9,13},{10,... | collective-permute-start | bytes 688136 | tf_op jit(solution)/shard_map/ppermute | solution.py:426
  31.1 9.8 %collective-permute-start.6 = (bf16[64,1792]{1,0:T(8,128)(2,1)S(1)}, bf16[64,1792]{1,0:T(8,128)(2,1)S(1)}, u32[]{:S(2)}, u32[]{:S(2)}) collective-permute-start(bf16[64,1792]{1,0:T(8,128)(2,1)S(1)} %collective-permute-done.5.refs_1_), channel_id=1, source_target_pairs={{0,1},{1,0},{2,3},{3,2},{4,5},{5,4},{6,7},{7,6},{8,9},{9,8},{10,11... | collective-permute-start | bytes 688136 | tf_op jit(solution)/shard_map/ppermute | solution.py:426
  31.1 4.6 %collective-permute-start = (s32[5,64]{1,0:T(8,128)S(1)}, s32[5,64]{1,0:T(8,128)S(1)}, u32[]{:S(2)}, u32[]{:S(2)}) collective-permute-start(s32[5,64]{1,0:T(8,128)S(1)} %get-tuple-element.14.meta.refs_0_), channel_id=1, source_target_pairs={{0,2},{1,3},{2,0},{3,1},{4,6},{5,7},{6,4},{7,5},{8,10},{9,11},{10,... | collective-permute-start | bytes 3848 | tf_op jit(solution)/shard_map/ppermute | solution.py:426
  31.6 8.6 %collective-permute-start.13 = (bf16[32,1792]{1,0:T(8,128)(2,1)S(1)}, bf16[32,1792]{1,0:T(8,128)(2,1)S(1)}, u32[]{:S(2)}, u32[]{:S(2)}) collective-permute-start(bf16[32,1792]{1,0:T(8,128)(2,1)S(1)} %collective-permute-done.7.refs_3_), channel_id=1, source_target_pairs={{0,8},{1,9},{2,10},{3,11},{4,12},{5,13},{6,14},{7,15},{8,0},{9,1},... | collective-permute-start | bytes 344072 | tf_op jit(solution)/shard_map/ppermute | solution.py:426
  35.7 5.2 %collective-permute-start.8 = (bf16[32,1792]{1,0:T(8,128)(2,1)S(1)}, bf16[32,1792]{1,0:T(8,128)(2,1)S(1)}, u32[]{:S(2)}, u32[]{:S(2)}) collective-permute-start(bf16[32,1792]{1,0:T(8,128)(2,1)S(1)} %collective-permute-done.7.refs_3_), channel_id=1, source_target_pairs={{0,1},{1,0},{2,3},{3,2},{4,5},{5,4},{6,7},{7,6},{8,9},{9,8},{10,11... | collective-permute-start | bytes 344072 | tf_op jit(solution)/shard_map/ppermute | solution.py:426
  40.2 6.2 %collective-permute-start.14 = (bf16[32,1792]{1,0:T(8,128)(2,1)S(1)}, bf16[32,1792]{1,0:T(8,128)(2,1)S(1)}, u32[]{:S(2)}, u32[]{:S(2)}) collective-permute-start(bf16[32,1792]{1,0:T(8,128)(2,1)S(1)} %collective-permute-done.13.refs_5_), channel_id=1, source_target_pairs={{0,1},{1,0},{2,3},{3,2},{4,5},{5,4},{6,7},{7,6},{8,9},{9,8},{10,11... | collective-permute-start | bytes 344072 | tf_op jit(solution)/shard_map/ppermute | solution.py:426
  40.2 6.2 %collective-permute-start.12 = (bf16[64,1792]{1,0:T(8,128)(2,1)S(1)}, bf16[64,1792]{1,0:T(8,128)(2,1)S(1)}, u32[]{:S(2)}, u32[]{:S(2)}) collective-permute-start(bf16[64,1792]{1,0:T(8,128)(2,1)S(1)} %collective-permute-done.11.refs_3_), channel_id=1, source_target_pairs={{0,1},{1,0},{2,3},{3,2},{4,5},{5,4},{6,7},{7,6},{8,9},{9,8},{10,11... | collective-permute-start | bytes 688136 | tf_op jit(solution)/shard_map/ppermute | solution.py:426
  40.8 5.7 %collective-permute-start.10 = (bf16[64,1792]{1,0:T(8,128)(2,1)S(1)}, bf16[64,1792]{1,0:T(8,128)(2,1)S(1)}, u32[]{:S(2)}, u32[]{:S(2)}) collective-permute-start(bf16[64,1792]{1,0:T(8,128)(2,1)S(1)} %collective-permute-done.9.refs_1_), channel_id=1, source_target_pairs={{0,1},{1,0},{2,3},{3,2},{4,5},{5,4},{6,7},{7,6},{8,9},{9,8},{10,11... | collective-permute-start | bytes 688136 | tf_op jit(solution)/shard_map/ppermute | solution.py:426

commit v2 on v1

--- a/solution.py
+++ b/solution.py
@@ -69,8 +69,8 @@
 
 
 def prep_kernel(
-    count, slots_in, targets_in, lengths_in, rewards_in, queries, residual, weight, gain, head,
-    slots, q_out, r_out, meta_out, weight_out, gain_out, head_out,
+    slots_in, targets_in, lengths_in, rewards_in, queries, residual, weight, gain,
+    slots, q_out, r_out, meta_out, weight_out, gain_out,
     targets, lengths, rewards, q_in, r_in, sems,
 ):
     samples, block, width = queries.shape
@@ -79,13 +79,10 @@
     cap = r_out.shape[0] // samples
     seq_at = lax.axis_index("seq")
     lanes = meta_out.shape[1]
-    step = head.shape[0] // count
     moves = [
         (slots_in, slots), (targets_in, targets), (lengths_in, lengths), (rewards_in, rewards),
         (queries, q_in), (residual, r_in), (weight, weight_out), (gain, gain_out.at[0]),
     ]
-    for n in range(count):
-        moves.append((head.at[pl.ds(n * step, step), :], head_out.at[pl.ds(n * step, step), :]))
     copies = [pltpu.make_async_copy(a, b, sems.at[n]) for n, (a, b) in enumerate(moves)]
     for copy in copies:
         copy.start()
@@ -102,11 +99,9 @@
         spot = iota((total, length), 1) == column
         found = jnp.sum(jnp.where(spot, targets[i : i + 1, :], 0), axis=1, keepdims=True)
         wanted = jnp.sum(jnp.where(eye, found, 0), axis=0, keepdims=True)
-        wanted = jnp.where((row >= 0) & (row < lengths[i]), wanted, -1)
-        for n in range(total // cap):
-            meta_out[n : n + 1, i * cap : (i + 1) * cap] = wanted[:, n * cap : (n + 1) * cap]
+        meta_out[i : i + 1, :] = jnp.where((row >= 0) & (row < lengths[i]), wanted, -1)
         reward_row = jnp.where(iota((1, lanes), 1) == i, rewards[i], reward_row)
-    meta_out[total // cap : total // cap + 1, :] = reward_row
+    meta_out[samples : samples + 1, :] = reward_row
     copies[4].wait()
     for i in range(samples):
         picked = jnp.dot(onehots[i], q_in[i], preferred_element_type=F32).astype(BF16)
@@ -164,6 +159,90 @@
     out[...] = jnp.dot(attended, weight[...], preferred_element_type=F32).astype(BF16)
 
 
+def parcel_kernel(flips, slots_in, keys, values, queries, residual, *refs):
+    outs, (slots, q_in, r_in, sems) = refs[: len(flips)], refs[len(flips) :]
+    samples, block, _ = queries.shape
+    half = r_in.shape[2]
+    seq_at = lax.axis_index("seq")
+    cap = slots.shape[1] // samples
+    start = pl.multiple_of(lax.axis_index("vocab") * half, half)
+    moves = [
+        (slots_in, slots), (queries, q_in), (residual.at[:, :, pl.ds(start, half)], r_in),
+    ]
+    for out, flip in zip(outs, flips):
+        taker = jnp.bitwise_xor(seq_at, flip)
+        moves.append((keys.at[taker], out.at[pl.ds(0, block), :]))
+        moves.append((values.at[taker], out.at[pl.ds(block, block), :]))
+    copies = [pltpu.make_async_copy(a, b, sems.at[n]) for n, (a, b) in enumerate(moves)]
+    for copy in copies:
+        copy.start()
+    copies[0].wait()
+    onehots = []
+    for flip in flips:
+        row = slots[pl.ds(jnp.bitwise_xor(seq_at, flip), 1), :]
+        local = jnp.clip(own_slot_column(row, seq_at, cap) - seq_at * block, 0, block - 1)
+        onehots.append((iota((cap, block), 1) == local).astype(F32).astype(BF16))
+    first = 2 * block
+    for copy, held in zip(copies[1:3], (q_in, r_in)):
+        copy.wait()
+        for out, flip, onehot in zip(outs, flips, onehots):
+            source = held[jnp.bitwise_xor(seq_at, flip)]
+            picked = jnp.dot(onehot, source, preferred_element_type=F32).astype(BF16)
+            for h in range(picked.shape[1] // HD):
+                out[first + h * cap : first + (h + 1) * cap, :] = picked[:, h * HD : (h + 1) * HD]
+        first += q_in.shape[2] // HD * cap
+    for copy in copies[3:]:
+        copy.wait()
+
+
+def completion_kernel(flips, block, slots, weight, *refs):
+    parcels, (out, residual, attended) = refs[: len(flips)], refs[len(flips) :]
+    heads = weight.shape[0] // HD
+    seq_at = lax.axis_index("seq")
+    cap = attended.shape[0] // len(flips)
+    row = slots[pl.ds(seq_at, 1), :]
+    owners = [jnp.bitwise_xor(seq_at, flip) for flip in flips]
+    span = block * len(flips)
+    lane = iota((1, span), 1)
+    key_pos = jnp.zeros((1, span), jnp.int32)
+    reach = []
+    for n, owner in enumerate(owners):
+        key_pos = jnp.where(lane // block == n, lane + (owner - n) * block, key_pos)
+        reach += [jnp.maximum(own_slot_column(row, owner, cap), 0)] * heads
+    first = 2 * block
+    last = first + heads * cap
+    keys = jnp.concatenate([p[:block, :] for p in parcels], axis=0)
+    values = jnp.concatenate([p[block:first, :] for p in parcels], axis=0)
+    query = jnp.concatenate([p[first:last, :] for p in parcels], axis=0)
+    scores = lax.dot_general(
+        query, keys, (((1,), (1,)), ((), ())), preferred_element_type=F32
+    ) * HD ** (-0.5)
+    allowed = key_pos <= jnp.concatenate(reach, axis=0)
+    scores = jnp.where(allowed, scores, FLOOR)
+    top = jnp.max(scores, axis=1, keepdims=True)
+    weights = jnp.where(allowed, jnp.exp(scores - top), 0.0)
+    total = jnp.sum(weights, axis=1, keepdims=True)
+    mixed = jnp.dot(weights.astype(BF16), values, preferred_element_type=F32)
+    mixed = (mixed / total).astype(BF16)
+    for n, (owner, parcel) in enumerate(zip(owners, parcels)):
+        spot = pl.ds(pl.multiple_of(owner * cap, cap), cap)
+        begin = n * heads * cap
+        attended[spot, :] = jnp.concatenate(
+            [mixed[begin + h * cap : begin + (h + 1) * cap, :] for h in range(heads)], axis=1
+        )
+        count = residual.shape[1] // HD
+        residual[spot, :] = jnp.concatenate(
+            [parcel[last + h * cap : last + (h + 1) * cap, :] for h in range(count)], axis=1
+        )
+    out[...] = jnp.dot(attended[...], weight[...], preferred_element_type=F32).astype(BF16)
+
+
+def pair_norm_kernel(mine, other, half_mine, half_other, gain, full, half):
+    low = jnp.concatenate([half_mine[...], half_other[...]], axis=1)
+    high = jnp.concatenate([half_other[...], half_mine[...]], axis=1)
+    norm_kernel(mine, other, jnp.where(lax.axis_index("vocab") == 0, low, high), gain, full, half)
+
+
 def norm_kernel(mine, other, residual, gain, full, half):
     hidden = residual[...].astype(F32) + (mine[...].astype(F32) + other[...].astype(F32))
     power = jnp.mean(hidden * hidden, axis=-1, keepdims=True)
@@ -340,9 +419,7 @@
 def close_kernel(relative, columns, length, stats, *refs):
     metas, (tokens_out, scores_out, advantages_out, objective_out, tokens) = refs[:-5], refs[-5:]
     samples, cap = tokens_out.shape
-    rows = samples * cap
-    chips = tokens.shape[0]
-    blocks = chips // columns
+    slots = tokens.shape[1]
     prompts = samples * columns
     where, seq_at = lax.axis_index("sample"), lax.axis_index("seq")
     metas = [ref[...] for ref in metas]
@@ -356,17 +433,17 @@
     for s in range(1, stats.shape[0]):
         total += jnp.exp(stats[s] - top)
         pick += stats[s]
-    logprob = pick[:, rows:] - (top + jnp.log(total))[:, :rows]
-    wanted = jnp.concatenate([meta[:blocks] for meta in metas], axis=0)
+    logprob = pick[:, slots:] - (top + jnp.log(total))[:, :slots]
+    wanted = jnp.concatenate([meta[:samples] for meta in metas], axis=0)
     tokens[...] = jnp.where(wanted >= 0, logprob, 0.0)
-    paid = [meta[blocks : blocks + 1, :].astype(F32) for meta in metas]
+    paid = [meta[samples : samples + 1, :].astype(F32) for meta in metas]
     reward_sum = functools.reduce(lambda a, b: a + b, [jnp.sum(row) for row in paid])
-    lane = iota((1, rows), 1)
+    lane = iota((1, slots), 1)
     objective = jnp.float32(0)
     for k in range(columns):
-        summed = jnp.sum(tokens[k * blocks : (k + 1) * blocks, :], axis=0, keepdims=True)
         for i in range(samples):
-            score = jnp.sum(summed[:, i * cap : (i + 1) * cap]) / length
+            at = k * samples + i
+            score = jnp.sum(tokens[at : at + 1, :]) / length
             reward = jnp.sum(jnp.where(lane == i, paid[k], 0.0))
             advantage = reward - (reward_sum - reward) / (prompts - 1)
             objective += advantage * score
@@ -377,9 +454,13 @@
                 advantages_out[i] = advantage
 
     objective_out[0] = -(objective / prompts)
-    mine = tokens[pl.ds(where * blocks + seq_at, 1), :]
-    for i in range(samples):
-        tokens_out[i : i + 1, :] = mine[:, i * cap : (i + 1) * cap]
+    mine = tokens[:samples, :]
+    for k in range(1, columns):
+        mine = jnp.where(where == k, tokens[k * samples : (k + 1) * samples, :], mine)
+    piece = mine[:, :cap]
+    for n in range(1, slots // cap):
+        piece = jnp.where(seq_at == n, mine[:, n * cap : (n + 1) * cap], piece)
+    tokens_out[...] = piece
 
 
 def close(stats, metas, relative, samples, cap, length):
@@ -396,7 +477,7 @@
         [stats, *metas],
         [vmem()] * (1 + len(metas)),
         out_specs=(vmem(), smem(), smem(), smem()),
-        scratch=[pltpu.VMEM((stats.shape[1], samples * cap), F32)],
+        scratch=[pltpu.VMEM((stats.shape[1], stats.shape[2] // 2), F32)],
     )
 
 
@@ -411,7 +492,7 @@
     length = targets.shape[1]
     rows = samples * cap
     sizes = tuple(lax.axis_size(axis) for axis in ("groups",) + CELL)
-    short = sizes == (2, 4, 2, 2) and samples % 2 == 0
+    short = sizes == (2, 4, 2, 2) and samples == seq_size and key_states.shape[2] == HD
 
     def send(array, target):
         pairs = []
@@ -441,74 +522,100 @@
     def beside(array):
         return send(array, lambda z, x, c: (z, x ^ 1, c))
 
-    kv_shape = (samples, block, 2 * key_states.shape[2])
-    pair = call(
-        pack_kernel,
-        jax.ShapeDtypeStruct(kv_shape, BF16),
-        [keep(key_states), keep(value_states)],
-        [hbm(), hbm()],
-        scratch=[pltpu.SemaphoreType.DMA((2,))],
-        limit=4,
-    )
+    flips = (0, 2, 3, 1)
     if short:
-        offsets = (0, 1, 3, 2)
-        far = send(pair, lambda z, x, c: (z ^ 2, x, c))
-        near = send(pair, lambda z, x, c: (z ^ 1, x, c))
-        wrap = send(pair, lambda z, x, c: (z ^ 3, x, c))
-        blocks = [pair, near, wrap, far]
+        half_width = model_width // vocab_size
+        parcel_rows = 2 * block + (width + half_width) // HD * cap
+        parcels = call(
+            functools.partial(parcel_kernel, flips),
+            tuple(jax.ShapeDtypeStruct((parcel_rows, HD), BF16) for _ in flips),
+            [keep(a) for a in (scored_slots, key_states, value_states, queries, residual)],
+            [hbm()] * 5,
+            scratch=[
+                pltpu.VMEM(scored_slots.shape, jnp.int32),
+                pltpu.VMEM(queries.shape, BF16),
+                pltpu.VMEM((samples, block, half_width), BF16),
+                pltpu.SemaphoreType.DMA((3 + 2 * len(flips),)),
+            ],
+        )
+        far = send(parcels[1], lambda z, x, c: (z ^ 2, x, c))
+        wrap = send(parcels[2], lambda z, x, c: (z ^ 3, x, c))
+        near = send(parcels[3], lambda z, x, c: (z ^ 1, x, c))
+        blocks = [parcels[0], far, wrap, near]
     else:
         offsets = (0,)
+        kv_shape = (samples, block, 2 * key_states.shape[2])
+        pair = call(
+            pack_kernel,
+            jax.ShapeDtypeStruct(kv_shape, BF16),
+            [keep(key_states), keep(value_states)],
+            [hbm(), hbm()],
+            scratch=[pltpu.SemaphoreType.DMA((2,))],
+            limit=4,
+        )
         blocks = [lax.all_gather(pair, "seq", axis=1, tiled=True)]
     heads = width // HD
-    count = 10 if vocab_head.shape[0] % 160 == 0 else 1
-    slots, picked, picked_resid, meta, weight, gain, head = call(
-        functools.partial(prep_kernel, count),
+    slots, picked, picked_resid, meta, weight, gain = call(
+        prep_kernel,
         (
             jax.ShapeDtypeStruct(scored_slots.shape, jnp.int32),
             jax.ShapeDtypeStruct((samples, heads * cap, HD), BF16),
             jax.ShapeDtypeStruct((rows, model_width), BF16),
-            jax.ShapeDtypeStruct((seq_size + 1, rows), jnp.int32),
+            jax.ShapeDtypeStruct((samples + 1, scored_slots.shape[1]), jnp.int32),
             pltpu.VMEM(out_weight.shape, BF16),
             pltpu.VMEM((1, model_width), F32),
-            pltpu.VMEM(vocab_head.shape, BF16),
         ),
         [
             keep(array)
             for array in (
                 scored_slots, targets, lengths, rewards, queries, residual,
-                out_weight, norm_gain, vocab_head,
+                out_weight, norm_gain,
             )
         ],
-        [hbm()] * 9,
+        [hbm()] * 8,
         scratch=[
             pltpu.VMEM(targets.shape, jnp.int32),
             pltpu.SMEM(lengths.shape, jnp.int32),
             pltpu.SMEM(rewards.shape, jnp.int32),
             pltpu.VMEM(queries.shape, BF16),
             pltpu.VMEM(residual.shape, BF16),
-            pltpu.SemaphoreType.DMA((8 + count,)),
+            pltpu.SemaphoreType.DMA((8,)),
         ],
         limit=12,
     )
-    head = pltpu.with_memory_space_constraint(head, pltpu.VMEM)
+    head = pltpu.with_memory_space_constraint(vocab_head, pltpu.VMEM)
     weight = pltpu.with_memory_space_constraint(weight, pltpu.VMEM)
-    partial_value = call(
-        functools.partial(attend_kernel, offsets),
-        jax.ShapeDtypeStruct((rows, model_width), BF16),
-        [slots, picked, weight, *blocks],
-        [vmem()] * (3 + len(blocks)),
-    )
+    if short:
+        partial_value, half_resid = call(
+            functools.partial(completion_kernel, flips, block),
+            (
+                jax.ShapeDtypeStruct((rows, model_width), BF16),
+                jax.ShapeDtypeStruct((rows, half_width), BF16),
+            ),
+            [slots, weight, *blocks],
+            [vmem()] * (2 + len(blocks)),
+            scratch=[pltpu.VMEM((rows, width), BF16)],
+            flops=10**10,
+        )
+    else:
+        partial_value = call(
+            functools.partial(attend_kernel, offsets),
+            jax.ShapeDtypeStruct((rows, model_width), BF16),
+            [slots, picked, weight, *blocks],
+            [vmem()] * (3 + len(blocks)),
+        )
     if short:
         other_meta = beside(meta)
         other_partial = across(partial_value)
+        other_resid = across(half_resid)
         normed, half = call(
-            norm_kernel,
+            pair_norm_kernel,
             (
                 jax.ShapeDtypeStruct((rows, model_width), BF16),
                 jax.ShapeDtypeStruct((rows // 2, model_width), BF16),
             ),
-            [partial_value, other_partial, picked_resid, gain],
-            [vmem()] * 4,
+            [partial_value, other_partial, half_resid, other_resid, gain],
+            [vmem()] * 5,
         )
         split = send(normed, lambda z, x, c: (z ^ (1, 3)[c], x, c))
         side = beside(half)
@@ -542,11 +649,17 @@
     every = lax.all_gather(normed, "seq", axis=0, tiled=True)
     every = lax.all_gather(every, "sample", axis=0, tiled=True)
     metas = lax.all_gather(meta, "sample", axis=0)
-    logs, picks = tiled_scores(head, every, metas[:, :seq_size].reshape(1, -1))
+    by_chip = (sample_size, samples, seq_size, cap)
+    wanted = metas[:, :samples].reshape(by_chip).transpose(0, 2, 1, 3).reshape(1, -1)
+    logs, picks = tiled_scores(vocab_head, every, wanted)
     top = lax.pmax(logs, CELL)
     total, pick = lax.psum((jnp.exp(logs - top), picks), CELL)
-    logs = (top + jnp.log(total)).reshape(1, -1, rows)
-    stats = jnp.concatenate([logs, pick.reshape(1, -1, rows)], axis=2)
+    by_row = (sample_size, seq_size, samples, cap)
+    stats = [
+        part.reshape(by_row).transpose(0, 2, 1, 3).reshape(1, sample_size * samples, seq_size * cap)
+        for part in (top + jnp.log(total), pick)
+    ]
+    stats = jnp.concatenate(stats, axis=2)
     metas = [metas[k] for k in range(sample_size)]
     return close(stats, metas, False, samples, cap, length)
 

time: 64.8 us -> 62.9 us (0.971)
  Pallas kernels: 22.5 us -> 18.7 us
  waiting for transfers between devices: 14 us -> 16.7 us
  starting transfers between devices: 15.9 us -> 15.1 us
    pallas_call x7, Pallas kernels: 22.5 us -> 18.7 us  [call(): pl.pallas_call(body, cost_estimate=cost, out_shape=outs, in_specs=in_spec...]
    ppermute x14 -> x15, waiting for transfers between devices: 14 us -> 16.7 us  [send(): return lax.ppermute(array, CELL, pairs)]
    ppermute x14 -> x15, starting transfers between devices: 14.4 us -> 13.5 us  [send(): return lax.ppermute(array, CELL, pairs)]
  transfers between devices with their start and end apart: 15 -> 16, of which waited for: 6 -> 6; matrix products, arithmetic and copies ran while one was open for 0% -> 0% of each run, Pallas kernels for 21% -> 14%
where the time goes in v2:
time: 62.9 us; the launch traced here: 62.7 us
  Pallas kernels  18.7 us (30%)
  waiting for transfers between devices  16.7 us (27%)
  starting transfers between devices  15.1 us (24%)
  blocking collectives  11.6 us (18%)
  between operations  0.74 us (1%)
    pallas_call x7, Pallas kernels, call(): pl.pallas_call(body, cost_estimate=cost, out_shape=outs, in_specs=in_spec...  18.7 us
    ppermute x15, waiting for transfers between devices, send(): return lax.ppermute(array, CELL, pairs)  16.7 us
    ppermute x15, starting transfers between devices, send(): return lax.ppermute(array, CELL, pairs)  13.5 us
    all_to_all x1, blocking collectives, steps(): stats = lax.all_to_all(stats, CELL, 0, 0, tiled=True)  11.6 us
    ppermute x1, starting transfers between devices, aside(): return lax.ppermute(array, ('groups',) + CELL, pairs)  1.62 us
  transfers between devices with their start and end apart: 16, of which 6 were waited for; matrix products, arithmetic and copies ran while one was open for 0% of the time, Pallas kernels for 14%

profile of v2, /device:TPU:0, one launch (start us, length us, event | category | flops | bytes accessed | tf_op | source)
XLA Modules:
  0.0 62.7 jit_solution(13788872244018954244)
XLA Ops:
  0.6 1.5 %shard_map.139 = (bf16[352,128]{1,0:T(8,128)(2,1)S(1)}, bf16[352,128]{1,0:T(8,128)(2,1)S(1)}, bf16[352,128]{1,0:T(8,128)(2,1)S(1)}, bf16[352,128]{1,0:T(8,128)(2,1)S(1)}) custom-call(s32[4,64]{1,0:T(4,128)} %slots_in.3, bf16[4,64,128]{2,1,0:T(8,128)(2,1)} %keys.1, bf16[4,64,128]{2,1,0:T(8,128)(2,1)} %values.1, bf16[4,64,896]{2,1,0:T(8,128)(2,1)} %queries.3, ...), custom_call_target="tpu_custom_call" | custom-call | tf_op jit(solution)/shard_map/pallas_call | solution.py:38
  2.2 4.1 %collective-permute-start.1 = (bf16[352,128]{1,0:T(8,128)(2,1)S(1)}, bf16[352,128]{1,0:T(8,128)(2,1)S(1)}, u32[]{:S(2)}, u32[]{:S(2)}) collective-permute-start(bf16[352,128]{1,0:T(8,128)(2,1)S(1)} %get-tuple-element.20), channel_id=1, source_target_pairs={{0,8},{1,9},{2,10},{3,11},{4,12},{5,13},{6,14},{7,15},{8,0},{9,1},... | collective-permute-start | bytes 270344 | tf_op jit(solution)/shard_map/ppermute | solution.py:507
  6.3 1.3 %collective-permute-start.2 = (bf16[352,128]{1,0:T(8,128)(2,1)S(1)}, bf16[352,128]{1,0:T(8,128)(2,1)S(1)}, u32[]{:S(2)}, u32[]{:S(2)}) collective-permute-start(bf16[352,128]{1,0:T(8,128)(2,1)S(1)} %get-tuple-element.21), channel_id=1, source_target_pairs={{0,12},{1,13},{2,14},{3,15},{4,8},{5,9},{6,10},{7,11},{8,4},{9,5},... | collective-permute-start | bytes 270344 | tf_op jit(solution)/shard_map/ppermute | solution.py:507
  7.7 0.2 collective-permute-start.3
  7.9 0.0 slice-start
  7.9 3.3 %shard_map.138 = (s32[4,64]{1,0:T(4,128)S(1)}, bf16[4,112,128]{2,1,0:T(8,128)(2,1)}, bf16[64,1792]{1,0:T(8,128)(2,1)}, s32[5,64]{1,0:T(8,128)S(1)}, bf16[896,179...) custom-call(s32[4,64]{1,0:T(4,128)} %slots_in.3, s32[4,256]{1,0:T(4,128)} %targets_in.1, s32[4]{0:T(128)} %lengths_in.1, ...), custom_call_target="tpu_custom_call" | custom-call | tf_op jit(solution)/shard_map/pallas_call | solution.py:38
  11.2 2.3 %collective-permute-done.1.refs_1_ = bf16[352,128]{1,0:T(8,128)(2,1)S(1)} collective-permute-done((bf16[352,128]{1,0:T(8,128)(2,1)S(1)}, bf16[352,128]{1,0:T(8,128)(2,1)S(1)}, u32[]{:S(2)}, u32[]{:S(2)}) %collective-permute-start.1) | collective-permute-done | bytes 90144 | tf_op jit(solution)/shard_map/ppermute | solution.py:507
  13.5 0.0 collective-permute-done.2.refs_2_
  13.5 0.6 collective-permute-done.3.refs_3_
  14.1 0.0 slice-start.1
  14.1 0.0 slice-start.2
  14.1 1.3 %shard_map.140 = (bf16[64,1792]{1,0:T(8,128)(2,1)S(1)}, bf16[64,896]{1,0:T(8,128)(2,1)S(1)}) custom-call(s32[4,64]{1,0:T(4,128)S(1)} %get-tuple-element.17.slots, bf16[896,1792]{1,0:T(8,128)(2,1)S(1)} %get-tuple-element.18.weight, bf16[352,128]{1,0:T(8,128)(2,1)S(1)} %get-tuple-element.19.refs_0_, bf16[352,128]{1,0:T(8,128)(2,1)S(1)} %collective-permute-done.1.refs_1_, ...), custom_call_target="tpu_custom_call" | custom-call | flops 10000000000 | tf_op jit(solution)/shard_map/pallas_call | solution.py:38
  15.4 0.1 collective-permute-start.4
  15.5 0.5 collective-permute-start.5
  16.0 1.1 %collective-permute-done.5.half_other = bf16[64,896]{1,0:T(8,128)(2,1)S(1)} collective-permute-done((bf16[64,896]{1,0:T(8,128)(2,1)S(1)}, bf16[64,896]{1,0:T(8,128)(2,1)S(1)}, u32[]{:S(2)}, u32[]{:S(2)}) %collective-permute-start.5) | collective-permute-done | bytes 114720 | tf_op jit(solution)/shard_map/ppermute | solution.py:507
  17.1 0.0 collective-permute-done.4.other
  17.1 0.2 shard_map.141
  17.3 1.5 %collective-permute-start.6 = (bf16[64,1792]{1,0:T(8,128)(2,1)S(1)}, bf16[64,1792]{1,0:T(8,128)(2,1)S(1)}, u32[]{:S(2)}, u32[]{:S(2)}) collective-permute-start(bf16[64,1792]{1,0:T(8,128)(2,1)S(1)} %get-tuple-element.26.refs_0_), channel_id=1, source_target_pairs={{0,4},{1,13},{2,6},{3,15},{4,0},{5,9},{6,2},{7,11},{8,12},{9,5},{1... | collective-permute-start | bytes 688136 | tf_op jit(solution)/shard_map/ppermute | solution.py:507
  18.8 1.5 %collective-permute-start.8 = (bf16[32,1792]{1,0:T(8,128)(2,1)S(1)}, bf16[32,1792]{1,0:T(8,128)(2,1)S(1)}, u32[]{:S(2)}, u32[]{:S(2)}) collective-permute-start(bf16[32,1792]{1,0:T(8,128)(2,1)S(1)} %get-tuple-element.27), channel_id=1, source_target_pairs={{0,2},{1,3},{2,0},{3,1},{4,6},{5,7},{6,4},{7,5},{8,10},{9,11},{10,... | collective-permute-start | bytes 344072 | tf_op jit(solution)/shard_map/ppermute | solution.py:507
  20.3 5.6 %collective-permute-done.6.refs_1_ = bf16[64,1792]{1,0:T(8,128)(2,1)S(1)} collective-permute-done((bf16[64,1792]{1,0:T(8,128)(2,1)S(1)}, bf16[64,1792]{1,0:T(8,128)(2,1)S(1)}, u32[]{:S(2)}, u32[]{:S(2)}) %collective-permute-start.6) | collective-permute-done | bytes 229408 | tf_op jit(solution)/shard_map/ppermute | solution.py:507
  25.9 1.6 %collective-permute-start.12 = (bf16[64,1792]{1,0:T(8,128)(2,1)S(1)}, bf16[64,1792]{1,0:T(8,128)(2,1)S(1)}, u32[]{:S(2)}, u32[]{:S(2)}) collective-permute-start(bf16[64,1792]{1,0:T(8,128)(2,1)S(1)} %collective-permute-done.6.refs_1_), channel_id=1, source_target_pairs={{0,16},{1,3},{2,18},{3,1},{4,20},{5,7},{6,22},{7,5},{8,24},{9,11},... | collective-permute-start | bytes 688136 | tf_op jit(solution)/shard_map/ppermute | solution.py:517
  27.5 1.5 %collective-permute-start.10 = (bf16[64,1792]{1,0:T(8,128)(2,1)S(1)}, bf16[64,1792]{1,0:T(8,128)(2,1)S(1)}, u32[]{:S(2)}, u32[]{:S(2)}) collective-permute-start(bf16[64,1792]{1,0:T(8,128)(2,1)S(1)} %collective-permute-done.6.refs_1_), channel_id=1, source_target_pairs={{0,2},{1,5},{2,0},{3,7},{4,6},{5,1},{6,4},{7,3},{8,10},{9,13},{10,... | collective-permute-start | bytes 688136 | tf_op jit(solution)/shard_map/ppermute | solution.py:507
  29.0 0.0 collective-permute-start.7
  29.0 0.5 collective-permute-start
  29.5 0.0 collective-permute-done.8.refs_3_
  29.5 1.6 %collective-permute-start.14 = (bf16[32,1792]{1,0:T(8,128)(2,1)S(1)}, bf16[32,1792]{1,0:T(8,128)(2,1)S(1)}, u32[]{:S(2)}, u32[]{:S(2)}) collective-permute-start(bf16[32,1792]{1,0:T(8,128)(2,1)S(1)} %collective-permute-done.8.refs_3_), channel_id=1, source_target_pairs={{0,8},{1,9},{2,10},{3,11},{4,12},{5,13},{6,14},{7,15},{8,0},{9,1},... | collective-permute-start | bytes 344072 | tf_op jit(solution)/shard_map/ppermute | solution.py:507
  31.2 2.5 %collective-permute-done.other_meta.refs_1_ = s32[5,64]{1,0:T(8,128)S(1)} collective-permute-done((s32[5,64]{1,0:T(8,128)S(1)}, s32[5,64]{1,0:T(8,128)S(1)}, u32[]{:S(2)}, u32[]{:S(2)}) %collective-permute-start) | collective-permute-done | bytes 1312 | tf_op jit(solution)/shard_map/ppermute | solution.py:507
  33.6 0.0 collective-permute-start.9
  33.6 4.6 %collective-permute-done.14.refs_5_ = bf16[32,1792]{1,0:T(8,128)(2,1)S(1)} collective-permute-done((bf16[32,1792]{1,0:T(8,128)(2,1)S(1)}, bf16[32,1792]{1,0:T(8,128)(2,1)S(1)}, u32[]{:S(2)}, u32[]{:S(2)}) %collective-permute-start.14) | collective-permute-done | bytes 114720 | tf_op jit(solution)/shard_map/ppermute | solution.py:507
  38.2 0.0 collective-permute-start.15
  38.2 0.0 collective-permute-done.12.refs_3_
  38.2 0.5 collective-permute-start.13
  38.7 0.0 collective-permute-done.10.refs_1_
  38.7 0.1 collective-permute-start.11
  38.8 0.0 collective-permute-done.9.refs_4_
  38.8 0.0 collective-permute-done.7.refs_2_
  38.8 0.0 slice-done
  38.8 0.0 slice-done.1
  38.8 0.0 slice-done.2
  38.8 0.0 slice-done.3
  38.8 0.0 slice-done.4
  38.8 5.6 %shard_map.142.refs_0_ = f32[4,128]{1,0:T(4,128)S(1)} custom-call(bf16[5120,1792]{1,0:T(8,128)(2,1)S(1)} %bitcast.1, s32[5,64]{1,0:T(8,128)S(1)} %get-tuple-element.16.meta.refs_0_, s32[5,64]{1,0:T(8,128)S(1)} %collective-permute-done.other_meta.refs_1_, bf16[64,1792]{1,0:T(8,128)(2,1)S(1)} %get-tuple-element.26.refs_0_, ...), custom_call_target="tpu_custom_call" | custom-call | flops 4697620480 | tf_op jit(solution)/shard_map/pallas_call | solution.py:38
  44.5 0.0 collective-permute-done.15.refs_6_
  44.5 0.0 collective-permute-done.13.refs_4_
  44.5 0.0 collective-permute-done.11.refs_2_
  44.5 5.6 %shard_map.143 = f32[16,8,128]{2,1,0:T(8,128)S(1)} custom-call(bf16[5120,1792]{1,0:T(8,128)(2,1)S(1)} %bitcast.1, s32[5,64]{1,0:T(8,128)S(1)} %get-tuple-element.16.meta.refs_0_, s32[5,64]{1,0:T(8,128)S(1)} %collective-permute-done.other_meta.refs_1_, f32[4,128]{1,0:T(4,128)S(1)} %shard_map.142.refs_0_, ...), custom_call_target="tpu_custom_call" | custom-call | flops 4697620480 | tf_op jit(solution)/shard_map/pallas_call | solution.py:38
  50.1 11.6 %all_to_all.5.stats = f32[16,8,128]{2,1,0:T(8,128)S(1)} all-to-all(f32[16,8,128]{2,1,0:T(8,128)S(1)} %shard_map.143), channel_id=1, replica_groups=mesh['groups'=2,'seq'=4,'sample'=2,'vocab'=2] {'seq','sample','vocab'}, dimensions={0} | all-to-all | bytes 131072 | tf_op jit(solution)/shard_map/all_to_all | solution.py:640
  61.7 1.1 %shard_map.144 = (f32[4,16]{1,0:T(4,128)}, f32[4]{0:T(128)}, f32[4]{0:T(128)}, f32[1]{0:T(128)}) custom-call(f32[16,8,128]{2,1,0:T(8,128)S(1)} %all_to_all.5.stats, s32[5,64]{1,0:T(8,128)S(1)} %get-tuple-element.16.meta.refs_0_, s32[5,64]{1,0:T(8,128)S(1)} %collective-permute-done.other_meta.refs_1_), custom_call_target="tpu_custom_call" | custom-call | tf_op jit(solution)/shard_map/pallas_call | solution.py:38
  (3 shorter events, 0.0 us)
Async XLA Ops:
  2.2 11.4 %collective-permute-start.1 = (bf16[352,128]{1,0:T(8,128)(2,1)S(1)}, bf16[352,128]{1,0:T(8,128)(2,1)S(1)}, u32[]{:S(2)}, u32[]{:S(2)}) collective-permute-start(bf16[352,128]{1,0:T(8,128)(2,1)S(1)} %get-tuple-element.20), channel_id=1, source_target_pairs={{0,8},{1,9},{2,10},{3,11},{4,12},{5,13},{6,14},{7,15},{8,0},{9,1},... | collective-permute-start | bytes 270344 | tf_op jit(solution)/shard_map/ppermute | solution.py:507
  6.3 7.2 %collective-permute-start.2 = (bf16[352,128]{1,0:T(8,128)(2,1)S(1)}, bf16[352,128]{1,0:T(8,128)(2,1)S(1)}, u32[]{:S(2)}, u32[]{:S(2)}) collective-permute-start(bf16[352,128]{1,0:T(8,128)(2,1)S(1)} %get-tuple-element.21), channel_id=1, source_target_pairs={{0,12},{1,13},{2,14},{3,15},{4,8},{5,9},{6,10},{7,11},{8,4},{9,5},... | collective-permute-start | bytes 270344 | tf_op jit(solution)/shard_map/ppermute | solution.py:507
  7.7 6.4 %collective-permute-start.3 = (bf16[352,128]{1,0:T(8,128)(2,1)S(1)}, bf16[352,128]{1,0:T(8,128)(2,1)S(1)}, u32[]{:S(2)}, u32[]{:S(2)}) collective-permute-start(bf16[352,128]{1,0:T(8,128)(2,1)S(1)} %get-tuple-element.22), channel_id=1, source_target_pairs={{0,4},{1,5},{2,6},{3,7},{4,0},{5,1},{6,2},{7,3},{8,12},{9,13},{10,... | collective-permute-start | bytes 270344 | tf_op jit(solution)/shard_map/ppermute | solution.py:507
  7.9 30.9 %slice-start = ((s8[18350080]{0:T(1024)(128)(4,1)}), s8[4194304]{0:T(1024)(128)(4,1)S(1)}, s32[]{:S(2)}) async-start(s8[18350080]{0:T(1024)(128)(4,1)} %bitcast), calls=%async_computation.1 | async-start | bytes 8388608
  14.1 24.7 %slice-start.1 = ((s8[18350080]{0:T(1024)(128)(4,1)}), s8[4194304]{0:T(1024)(128)(4,1)S(1)}, s32[]{:S(2)}) async-start(s8[18350080]{0:T(1024)(128)(4,1)} %bitcast), calls=%async_computation.2 | async-start | bytes 8388608
  14.1 24.7 %slice-start.2 = ((s8[18350080]{0:T(1024)(128)(4,1)}), s8[4194304]{0:T(1024)(128)(4,1)S(1)}, s32[]{:S(2)}) async-start(s8[18350080]{0:T(1024)(128)(4,1)} %bitcast), calls=%async_computation.3 | async-start | bytes 8388608
  14.1 24.7 %slice-start.3 = ((s8[18350080]{0:T(1024)(128)(4,1)}), s8[4194304]{0:T(1024)(128)(4,1)S(1)}, s32[]{:S(2)}) async-start(s8[18350080]{0:T(1024)(128)(4,1)} %bitcast), calls=%async_computation.4 | async-start | bytes 8388608
  14.1 24.7 %slice-start.4 = ((s8[18350080]{0:T(1024)(128)(4,1)}), s8[1572864]{0:T(1024)(128)(4,1)S(1)}, s32[]{:S(2)}) async-start(s8[18350080]{0:T(1024)(128)(4,1)} %bitcast), calls=%async_computation.5 | async-start | bytes 3145728
  15.4 1.7 %collective-permute-start.4 = (bf16[64,1792]{1,0:T(8,128)(2,1)S(1)}, bf16[64,1792]{1,0:T(8,128)(2,1)S(1)}, u32[]{:S(2)}, u32[]{:S(2)}) collective-permute-start(bf16[64,1792]{1,0:T(8,128)(2,1)S(1)} %get-tuple-element.23.mine), channel_id=1, source_target_pairs={{0,1},{1,0},{2,3},{3,2},{4,5},{5,4},{6,7},{7,6},{8,9},{9,8},{10,11... | collective-permute-start | bytes 688136 | tf_op jit(solution)/shard_map/ppermute | solution.py:507
  15.5 1.6 %collective-permute-start.5 = (bf16[64,896]{1,0:T(8,128)(2,1)S(1)}, bf16[64,896]{1,0:T(8,128)(2,1)S(1)}, u32[]{:S(2)}, u32[]{:S(2)}) collective-permute-start(bf16[64,896]{1,0:T(8,128)(2,1)S(1)} %get-tuple-element.24.half_mine), channel_id=1, source_target_pairs={{0,1},{1,0},{2,3},{3,2},{4,5},{5,4},{6,7},{7,6},{8,9},{9,8},{10,11... | collective-permute-start | bytes 344072 | tf_op jit(solution)/shard_map/ppermute | solution.py:507
  17.3 8.5 %collective-permute-start.6 = (bf16[64,1792]{1,0:T(8,128)(2,1)S(1)}, bf16[64,1792]{1,0:T(8,128)(2,1)S(1)}, u32[]{:S(2)}, u32[]{:S(2)}) collective-permute-start(bf16[64,1792]{1,0:T(8,128)(2,1)S(1)} %get-tuple-element.26.refs_0_), channel_id=1, source_target_pairs={{0,4},{1,13},{2,6},{3,15},{4,0},{5,9},{6,2},{7,11},{8,12},{9,5},{1... | collective-permute-start | bytes 688136 | tf_op jit(solution)/shard_map/ppermute | solution.py:507
  18.8 10.7 %collective-permute-start.8 = (bf16[32,1792]{1,0:T(8,128)(2,1)S(1)}, bf16[32,1792]{1,0:T(8,128)(2,1)S(1)}, u32[]{:S(2)}, u32[]{:S(2)}) collective-permute-start(bf16[32,1792]{1,0:T(8,128)(2,1)S(1)} %get-tuple-element.27), channel_id=1, source_target_pairs={{0,2},{1,3},{2,0},{3,1},{4,6},{5,7},{6,4},{7,5},{8,10},{9,11},{10,... | collective-permute-start | bytes 344072 | tf_op jit(solution)/shard_map/ppermute | solution.py:507
  25.9 12.3 %collective-permute-start.12 = (bf16[64,1792]{1,0:T(8,128)(2,1)S(1)}, bf16[64,1792]{1,0:T(8,128)(2,1)S(1)}, u32[]{:S(2)}, u32[]{:S(2)}) collective-permute-start(bf16[64,1792]{1,0:T(8,128)(2,1)S(1)} %collective-permute-done.6.refs_1_), channel_id=1, source_target_pairs={{0,16},{1,3},{2,18},{3,1},{4,20},{5,7},{6,22},{7,5},{8,24},{9,11},... | collective-permute-start | bytes 688136 | tf_op jit(solution)/shard_map/ppermute | solution.py:517
  27.5 11.2 %collective-permute-start.10 = (bf16[64,1792]{1,0:T(8,128)(2,1)S(1)}, bf16[64,1792]{1,0:T(8,128)(2,1)S(1)}, u32[]{:S(2)}, u32[]{:S(2)}) collective-permute-start(bf16[64,1792]{1,0:T(8,128)(2,1)S(1)} %collective-permute-done.6.refs_1_), channel_id=1, source_target_pairs={{0,2},{1,5},{2,0},{3,7},{4,6},{5,1},{6,4},{7,3},{8,10},{9,13},{10,... | collective-permute-start | bytes 688136 | tf_op jit(solution)/shard_map/ppermute | solution.py:507
  29.0 9.8 %collective-permute-start.7 = (bf16[64,1792]{1,0:T(8,128)(2,1)S(1)}, bf16[64,1792]{1,0:T(8,128)(2,1)S(1)}, u32[]{:S(2)}, u32[]{:S(2)}) collective-permute-start(bf16[64,1792]{1,0:T(8,128)(2,1)S(1)} %collective-permute-done.6.refs_1_), channel_id=1, source_target_pairs={{0,1},{1,0},{2,3},{3,2},{4,5},{5,4},{6,7},{7,6},{8,9},{9,8},{10,11... | collective-permute-start | bytes 688136 | tf_op jit(solution)/shard_map/ppermute | solution.py:507
  29.0 4.6 %collective-permute-start = (s32[5,64]{1,0:T(8,128)S(1)}, s32[5,64]{1,0:T(8,128)S(1)}, u32[]{:S(2)}, u32[]{:S(2)}) collective-permute-start(s32[5,64]{1,0:T(8,128)S(1)} %get-tuple-element.16.meta.refs_0_), channel_id=1, source_target_pairs={{0,2},{1,3},{2,0},{3,1},{4,6},{5,7},{6,4},{7,5},{8,10},{9,11},{10,... | collective-permute-start | bytes 3848 | tf_op jit(solution)/shard_map/ppermute | solution.py:507
  29.5 8.6 %collective-permute-start.14 = (bf16[32,1792]{1,0:T(8,128)(2,1)S(1)}, bf16[32,1792]{1,0:T(8,128)(2,1)S(1)}, u32[]{:S(2)}, u32[]{:S(2)}) collective-permute-start(bf16[32,1792]{1,0:T(8,128)(2,1)S(1)} %collective-permute-done.8.refs_3_), channel_id=1, source_target_pairs={{0,8},{1,9},{2,10},{3,11},{4,12},{5,13},{6,14},{7,15},{8,0},{9,1},... | collective-permute-start | bytes 344072 | tf_op jit(solution)/shard_map/ppermute | solution.py:507
  33.6 5.2 %collective-permute-start.9 = (bf16[32,1792]{1,0:T(8,128)(2,1)S(1)}, bf16[32,1792]{1,0:T(8,128)(2,1)S(1)}, u32[]{:S(2)}, u32[]{:S(2)}) collective-permute-start(bf16[32,1792]{1,0:T(8,128)(2,1)S(1)} %collective-permute-done.8.refs_3_), channel_id=1, source_target_pairs={{0,1},{1,0},{2,3},{3,2},{4,5},{5,4},{6,7},{7,6},{8,9},{9,8},{10,11... | collective-permute-start | bytes 344072 | tf_op jit(solution)/shard_map/ppermute | solution.py:507
  38.2 6.3 %collective-permute-start.15 = (bf16[32,1792]{1,0:T(8,128)(2,1)S(1)}, bf16[32,1792]{1,0:T(8,128)(2,1)S(1)}, u32[]{:S(2)}, u32[]{:S(2)}) collective-permute-start(bf16[32,1792]{1,0:T(8,128)(2,1)S(1)} %collective-permute-done.14.refs_5_), channel_id=1, source_target_pairs={{0,1},{1,0},{2,3},{3,2},{4,5},{5,4},{6,7},{7,6},{8,9},{9,8},{10,11... | collective-permute-start | bytes 344072 | tf_op jit(solution)/shard_map/ppermute | solution.py:507
  38.2 6.3 %collective-permute-start.13 = (bf16[64,1792]{1,0:T(8,128)(2,1)S(1)}, bf16[64,1792]{1,0:T(8,128)(2,1)S(1)}, u32[]{:S(2)}, u32[]{:S(2)}) collective-permute-start(bf16[64,1792]{1,0:T(8,128)(2,1)S(1)} %collective-permute-done.12.refs_3_), channel_id=1, source_target_pairs={{0,1},{1,0},{2,3},{3,2},{4,5},{5,4},{6,7},{7,6},{8,9},{9,8},{10,11... | collective-permute-start | bytes 688136 | tf_op jit(solution)/shard_map/ppermute | solution.py:507
  38.7 5.8 %collective-permute-start.11 = (bf16[64,1792]{1,0:T(8,128)(2,1)S(1)}, bf16[64,1792]{1,0:T(8,128)(2,1)S(1)}, u32[]{:S(2)}, u32[]{:S(2)}) collective-permute-start(bf16[64,1792]{1,0:T(8,128)(2,1)S(1)} %collective-permute-done.10.refs_1_), channel_id=1, source_target_pairs={{0,1},{1,0},{2,3},{3,2},{4,5},{5,4},{6,7},{7,6},{8,9},{9,8},{10,11... | collective-permute-start | bytes 688136 | tf_op jit(solution)/shard_map/ppermute | solution.py:507

commit v3 on v2

--- a/solution.py
+++ b/solution.py
@@ -196,7 +196,8 @@
 
 
 def completion_kernel(flips, block, slots, weight, *refs):
-    parcels, (out, residual, attended) = refs[: len(flips)], refs[len(flips) :]
+    parcels, (out, attended) = refs[: len(flips)], refs[len(flips) :]
+    width = weight.shape[1]
     heads = weight.shape[0] // HD
     seq_at = lax.axis_index("seq")
     cap = attended.shape[0] // len(flips)
@@ -230,17 +231,20 @@
         attended[spot, :] = jnp.concatenate(
             [mixed[begin + h * cap : begin + (h + 1) * cap, :] for h in range(heads)], axis=1
         )
-        count = residual.shape[1] // HD
-        residual[spot, :] = jnp.concatenate(
+        count = (out.shape[1] - width) // HD
+        out[spot, width:] = jnp.concatenate(
             [parcel[last + h * cap : last + (h + 1) * cap, :] for h in range(count)], axis=1
         )
-    out[...] = jnp.dot(attended[...], weight[...], preferred_element_type=F32).astype(BF16)
-
-
-def pair_norm_kernel(mine, other, half_mine, half_other, gain, full, half):
-    low = jnp.concatenate([half_mine[...], half_other[...]], axis=1)
-    high = jnp.concatenate([half_other[...], half_mine[...]], axis=1)
-    norm_kernel(mine, other, jnp.where(lax.axis_index("vocab") == 0, low, high), gain, full, half)
+    total = jnp.dot(attended[...], weight[...], preferred_element_type=F32)
+    out[:, :width] = total.astype(BF16)
+
+
+def pair_norm_kernel(mine, other, gain, full, half):
+    width = gain.shape[1]
+    low = jnp.concatenate([mine[:, width:], other[:, width:]], axis=1)
+    high = jnp.concatenate([other[:, width:], mine[:, width:]], axis=1)
+    residual = jnp.where(lax.axis_index("vocab") == 0, low, high)
+    norm_kernel(mine[:, :width], other[:, :width], residual, gain, full, half)
 
 
 def norm_kernel(mine, other, residual, gain, full, half):
@@ -586,12 +590,9 @@
     head = pltpu.with_memory_space_constraint(vocab_head, pltpu.VMEM)
     weight = pltpu.with_memory_space_constraint(weight, pltpu.VMEM)
     if short:
-        partial_value, half_resid = call(
+        partial_value = call(
             functools.partial(completion_kernel, flips, block),
-            (
-                jax.ShapeDtypeStruct((rows, model_width), BF16),
-                jax.ShapeDtypeStruct((rows, half_width), BF16),
-            ),
+            jax.ShapeDtypeStruct((rows, model_width + half_width), BF16),
             [slots, weight, *blocks],
             [vmem()] * (2 + len(blocks)),
             scratch=[pltpu.VMEM((rows, width), BF16)],
@@ -607,15 +608,14 @@
     if short:
         other_meta = beside(meta)
         other_partial = across(partial_value)
-        other_resid = across(half_resid)
         normed, half = call(
             pair_norm_kernel,
             (
                 jax.ShapeDtypeStruct((rows, model_width), BF16),
                 jax.ShapeDtypeStruct((rows // 2, model_width), BF16),
             ),
-            [partial_value, other_partial, half_resid, other_resid, gain],
-            [vmem()] * 5,
+            [partial_value, other_partial, gain],
+            [vmem()] * 3,
         )
         split = send(normed, lambda z, x, c: (z ^ (1, 3)[c], x, c))
         side = beside(half)

time: 62.9 us -> 62.9 us (level)
    ppermute x15 -> x14, starting transfers between devices: 13.5 us -> 12.9 us  [send(): return lax.ppermute(array, CELL, pairs)]
    ppermute x15 -> x14, waiting for transfers between devices: 16.7 us -> 17.2 us  [send(): return lax.ppermute(array, CELL, pairs)]
  transfers between devices with their start and end apart: 16 -> 15, of which waited for: 6 -> 6; matrix products, arithmetic and copies ran while one was open for 0% -> 0% of each run, Pallas kernels for 14% -> 14%
where the time goes in v3:
time: 62.9 us; the launch traced here: 62.7 us
  Pallas kernels  18.7 us (30%)
  waiting for transfers between devices  17.2 us (27%)
  starting transfers between devices  14.5 us (23%)
  blocking collectives  11.5 us (18%)
  between operations  0.74 us (1%)
    pallas_call x7, Pallas kernels, call(): pl.pallas_call(body, cost_estimate=cost, out_shape=outs, in_specs=in_spec...  18.7 us
    ppermute x14, waiting for transfers between devices, send(): return lax.ppermute(array, CELL, pairs)  17.2 us
    ppermute x14, starting transfers between devices, send(): return lax.ppermute(array, CELL, pairs)  12.9 us
    all_to_all x1, blocking collectives, steps(): stats = lax.all_to_all(stats, CELL, 0, 0, tiled=True)  11.5 us
    ppermute x1, starting transfers between devices, aside(): return lax.ppermute(array, ('groups',) + CELL, pairs)  1.62 us
  transfers between devices with their start and end apart: 15, of which 6 were waited for; matrix products, arithmetic and copies ran while one was open for 0% of the time, Pallas kernels for 14%

profile of v3, /device:TPU:0, one launch (start us, length us, event | category | flops | bytes accessed | tf_op | source)
XLA Modules:
  0.0 62.7 jit_solution(9423622097012487386)
XLA Ops:
  0.6 1.5 %shard_map.139 = (bf16[352,128]{1,0:T(8,128)(2,1)S(1)}, bf16[352,128]{1,0:T(8,128)(2,1)S(1)}, bf16[352,128]{1,0:T(8,128)(2,1)S(1)}, bf16[352,128]{1,0:T(8,128)(2,1)S(1)}) custom-call(s32[4,64]{1,0:T(4,128)} %slots_in.3, bf16[4,64,128]{2,1,0:T(8,128)(2,1)} %keys.1, bf16[4,64,128]{2,1,0:T(8,128)(2,1)} %values.1, bf16[4,64,896]{2,1,0:T(8,128)(2,1)} %queries.3, ...), custom_call_target="tpu_custom_call" | custom-call | tf_op jit(solution)/shard_map/pallas_call | solution.py:38
  2.2 4.1 %collective-permute-start.1 = (bf16[352,128]{1,0:T(8,128)(2,1)S(1)}, bf16[352,128]{1,0:T(8,128)(2,1)S(1)}, u32[]{:S(2)}, u32[]{:S(2)}) collective-permute-start(bf16[352,128]{1,0:T(8,128)(2,1)S(1)} %get-tuple-element.18), channel_id=1, source_target_pairs={{0,8},{1,9},{2,10},{3,11},{4,12},{5,13},{6,14},{7,15},{8,0},{9,1},... | collective-permute-start | bytes 270344 | tf_op jit(solution)/shard_map/ppermute | solution.py:511
  6.3 1.3 %collective-permute-start.2 = (bf16[352,128]{1,0:T(8,128)(2,1)S(1)}, bf16[352,128]{1,0:T(8,128)(2,1)S(1)}, u32[]{:S(2)}, u32[]{:S(2)}) collective-permute-start(bf16[352,128]{1,0:T(8,128)(2,1)S(1)} %get-tuple-element.19), channel_id=1, source_target_pairs={{0,12},{1,13},{2,14},{3,15},{4,8},{5,9},{6,10},{7,11},{8,4},{9,5},... | collective-permute-start | bytes 270344 | tf_op jit(solution)/shard_map/ppermute | solution.py:511
  7.7 0.2 collective-permute-start.3
  7.9 0.0 slice-start
  7.9 3.3 %shard_map.138 = (s32[4,64]{1,0:T(4,128)S(1)}, bf16[4,112,128]{2,1,0:T(8,128)(2,1)}, bf16[64,1792]{1,0:T(8,128)(2,1)}, s32[5,64]{1,0:T(8,128)S(1)}, bf16[896,179...) custom-call(s32[4,64]{1,0:T(4,128)} %slots_in.3, s32[4,256]{1,0:T(4,128)} %targets_in.1, s32[4]{0:T(128)} %lengths_in.1, ...), custom_call_target="tpu_custom_call" | custom-call | tf_op jit(solution)/shard_map/pallas_call | solution.py:38
  11.2 2.3 %collective-permute-done.1.refs_1_ = bf16[352,128]{1,0:T(8,128)(2,1)S(1)} collective-permute-done((bf16[352,128]{1,0:T(8,128)(2,1)S(1)}, bf16[352,128]{1,0:T(8,128)(2,1)S(1)}, u32[]{:S(2)}, u32[]{:S(2)}) %collective-permute-start.1) | collective-permute-done | bytes 90144 | tf_op jit(solution)/shard_map/ppermute | solution.py:511
  13.5 0.0 collective-permute-done.2.refs_2_
  13.5 0.6 collective-permute-done.3.refs_3_
  14.1 0.0 slice-start.1
  14.1 0.0 slice-start.2
  14.1 0.0 slice-start.3
  14.1 0.0 slice-start.4
  14.1 1.3 %shard_map.140.mine = bf16[64,2688]{1,0:T(8,128)(2,1)S(1)} custom-call(s32[4,64]{1,0:T(4,128)S(1)} %get-tuple-element.15.slots, bf16[896,1792]{1,0:T(8,128)(2,1)S(1)} %get-tuple-element.16.weight, bf16[352,128]{1,0:T(8,128)(2,1)S(1)} %get-tuple-element.17.refs_0_, bf16[352,128]{1,0:T(8,128)(2,1)S(1)} %collective-permute-done.1.refs_1_, ...), custom_call_target="tpu_custom_call" | custom-call | flops 10000000000 | tf_op jit(solution)/shard_map/pallas_call | solution.py:38
  15.4 0.1 collective-permute-start.4
  15.5 1.6 %collective-permute-done.4.other = bf16[64,2688]{1,0:T(8,128)(2,1)S(1)} collective-permute-done((bf16[64,2688]{1,0:T(8,128)(2,1)S(1)}, bf16[64,2688]{1,0:T(8,128)(2,1)S(1)}, u32[]{:S(2)}, u32[]{:S(2)}) %collective-permute-start.4) | collective-permute-done | bytes 344096 | tf_op jit(solution)/shard_map/ppermute | solution.py:511
  17.1 0.2 shard_map.141
  17.3 1.5 %collective-permute-start.5 = (bf16[64,1792]{1,0:T(8,128)(2,1)S(1)}, bf16[64,1792]{1,0:T(8,128)(2,1)S(1)}, u32[]{:S(2)}, u32[]{:S(2)}) collective-permute-start(bf16[64,1792]{1,0:T(8,128)(2,1)S(1)} %get-tuple-element.22.refs_0_), channel_id=1, source_target_pairs={{0,4},{1,13},{2,6},{3,15},{4,0},{5,9},{6,2},{7,11},{8,12},{9,5},{1... | collective-permute-start | bytes 688136 | tf_op jit(solution)/shard_map/ppermute | solution.py:511
  18.8 1.5 %collective-permute-start.7 = (bf16[32,1792]{1,0:T(8,128)(2,1)S(1)}, bf16[32,1792]{1,0:T(8,128)(2,1)S(1)}, u32[]{:S(2)}, u32[]{:S(2)}) collective-permute-start(bf16[32,1792]{1,0:T(8,128)(2,1)S(1)} %get-tuple-element.23), channel_id=1, source_target_pairs={{0,2},{1,3},{2,0},{3,1},{4,6},{5,7},{6,4},{7,5},{8,10},{9,11},{10,... | collective-permute-start | bytes 344072 | tf_op jit(solution)/shard_map/ppermute | solution.py:511
  20.3 5.6 %collective-permute-done.5.refs_1_ = bf16[64,1792]{1,0:T(8,128)(2,1)S(1)} collective-permute-done((bf16[64,1792]{1,0:T(8,128)(2,1)S(1)}, bf16[64,1792]{1,0:T(8,128)(2,1)S(1)}, u32[]{:S(2)}, u32[]{:S(2)}) %collective-permute-start.5) | collective-permute-done | bytes 229408 | tf_op jit(solution)/shard_map/ppermute | solution.py:511
  25.9 1.6 %collective-permute-start.11 = (bf16[64,1792]{1,0:T(8,128)(2,1)S(1)}, bf16[64,1792]{1,0:T(8,128)(2,1)S(1)}, u32[]{:S(2)}, u32[]{:S(2)}) collective-permute-start(bf16[64,1792]{1,0:T(8,128)(2,1)S(1)} %collective-permute-done.5.refs_1_), channel_id=1, source_target_pairs={{0,16},{1,3},{2,18},{3,1},{4,20},{5,7},{6,22},{7,5},{8,24},{9,11},... | collective-permute-start | bytes 688136 | tf_op jit(solution)/shard_map/ppermute | solution.py:521
  27.5 1.5 %collective-permute-start.9 = (bf16[64,1792]{1,0:T(8,128)(2,1)S(1)}, bf16[64,1792]{1,0:T(8,128)(2,1)S(1)}, u32[]{:S(2)}, u32[]{:S(2)}) collective-permute-start(bf16[64,1792]{1,0:T(8,128)(2,1)S(1)} %collective-permute-done.5.refs_1_), channel_id=1, source_target_pairs={{0,2},{1,5},{2,0},{3,7},{4,6},{5,1},{6,4},{7,3},{8,10},{9,13},{10,... | collective-permute-start | bytes 688136 | tf_op jit(solution)/shard_map/ppermute | solution.py:511
  29.0 0.0 collective-permute-start.6
  29.0 0.5 collective-permute-start
  29.5 0.0 collective-permute-done.7.refs_3_
  29.5 1.6 %collective-permute-start.13 = (bf16[32,1792]{1,0:T(8,128)(2,1)S(1)}, bf16[32,1792]{1,0:T(8,128)(2,1)S(1)}, u32[]{:S(2)}, u32[]{:S(2)}) collective-permute-start(bf16[32,1792]{1,0:T(8,128)(2,1)S(1)} %collective-permute-done.7.refs_3_), channel_id=1, source_target_pairs={{0,8},{1,9},{2,10},{3,11},{4,12},{5,13},{6,14},{7,15},{8,0},{9,1},... | collective-permute-start | bytes 344072 | tf_op jit(solution)/shard_map/ppermute | solution.py:511
  31.1 2.5 %collective-permute-done.other_meta.refs_1_ = s32[5,64]{1,0:T(8,128)S(1)} collective-permute-done((s32[5,64]{1,0:T(8,128)S(1)}, s32[5,64]{1,0:T(8,128)S(1)}, u32[]{:S(2)}, u32[]{:S(2)}) %collective-permute-start) | collective-permute-done | bytes 1312 | tf_op jit(solution)/shard_map/ppermute | solution.py:511
  33.6 0.0 collective-permute-start.8
  33.6 4.6 %collective-permute-done.13.refs_5_ = bf16[32,1792]{1,0:T(8,128)(2,1)S(1)} collective-permute-done((bf16[32,1792]{1,0:T(8,128)(2,1)S(1)}, bf16[32,1792]{1,0:T(8,128)(2,1)S(1)}, u32[]{:S(2)}, u32[]{:S(2)}) %collective-permute-start.13) | collective-permute-done | bytes 114720 | tf_op jit(solution)/shard_map/ppermute | solution.py:511
  38.2 0.0 collective-permute-start.14
  38.2 0.0 collective-permute-done.11.refs_3_
  38.2 0.5 collective-permute-start.12
  38.7 0.0 collective-permute-done.9.refs_1_
  38.7 0.1 collective-permute-start.10
  38.8 0.0 collective-permute-done.8.refs_4_
  38.8 0.0 collective-permute-done.6.refs_2_
  38.8 0.0 slice-done
  38.8 0.0 slice-done.1
  38.8 0.0 slice-done.2
  38.8 0.0 slice-done.3
  38.8 0.0 slice-done.4
  38.8 5.6 %shard_map.142.refs_0_ = f32[4,128]{1,0:T(4,128)S(1)} custom-call(bf16[5120,1792]{1,0:T(8,128)(2,1)S(1)} %bitcast.1, s32[5,64]{1,0:T(8,128)S(1)} %get-tuple-element.14.meta.refs_0_, s32[5,64]{1,0:T(8,128)S(1)} %collective-permute-done.other_meta.refs_1_, bf16[64,1792]{1,0:T(8,128)(2,1)S(1)} %get-tuple-element.22.refs_0_, ...), custom_call_target="tpu_custom_call" | custom-call | flops 4697620480 | tf_op jit(solution)/shard_map/pallas_call | solution.py:38
  44.5 0.0 collective-permute-done.14.refs_6_
  44.5 0.0 collective-permute-done.12.refs_4_
  44.5 0.0 collective-permute-done.10.refs_2_
  44.5 5.6 %shard_map.143 = f32[16,8,128]{2,1,0:T(8,128)S(1)} custom-call(bf16[5120,1792]{1,0:T(8,128)(2,1)S(1)} %bitcast.1, s32[5,64]{1,0:T(8,128)S(1)} %get-tuple-element.14.meta.refs_0_, s32[5,64]{1,0:T(8,128)S(1)} %collective-permute-done.other_meta.refs_1_, f32[4,128]{1,0:T(4,128)S(1)} %shard_map.142.refs_0_, bf16[64,1792]{1,0:T(8,128)(2,1)S(1)} %collective-permute-done.9.refs_1_, ...), custom_call_target="tpu_custom_call" | custom-call | flops 4697620480 | tf_op jit(solution)/shard_map/pallas_call | solution.py:38
  50.1 11.5 %all_to_all.5.stats = f32[16,8,128]{2,1,0:T(8,128)S(1)} all-to-all(f32[16,8,128]{2,1,0:T(8,128)S(1)} %shard_map.143), channel_id=1, replica_groups=mesh['groups'=2,'seq'=4,'sample'=2,'vocab'=2] {'seq','sample','vocab'}, dimensions={0} | all-to-all | bytes 131072 | tf_op jit(solution)/shard_map/all_to_all | solution.py:640
  61.6 1.1 %shard_map.144 = (f32[4,16]{1,0:T(4,128)}, f32[4]{0:T(128)}, f32[4]{0:T(128)}, f32[1]{0:T(128)}) custom-call(f32[16,8,128]{2,1,0:T(8,128)S(1)} %all_to_all.5.stats, s32[5,64]{1,0:T(8,128)S(1)} %get-tuple-element.14.meta.refs_0_, s32[5,64]{1,0:T(8,128)S(1)} %collective-permute-done.other_meta.refs_1_), custom_call_target="tpu_custom_call" | custom-call | tf_op jit(solution)/shard_map/pallas_call | solution.py:38
  (1 shorter events, 0.0 us)
Async XLA Ops:
  2.2 11.4 %collective-permute-start.1 = (bf16[352,128]{1,0:T(8,128)(2,1)S(1)}, bf16[352,128]{1,0:T(8,128)(2,1)S(1)}, u32[]{:S(2)}, u32[]{:S(2)}) collective-permute-start(bf16[352,128]{1,0:T(8,128)(2,1)S(1)} %get-tuple-element.18), channel_id=1, source_target_pairs={{0,8},{1,9},{2,10},{3,11},{4,12},{5,13},{6,14},{7,15},{8,0},{9,1},... | collective-permute-start | bytes 270344 | tf_op jit(solution)/shard_map/ppermute | solution.py:511
  6.3 7.2 %collective-permute-start.2 = (bf16[352,128]{1,0:T(8,128)(2,1)S(1)}, bf16[352,128]{1,0:T(8,128)(2,1)S(1)}, u32[]{:S(2)}, u32[]{:S(2)}) collective-permute-start(bf16[352,128]{1,0:T(8,128)(2,1)S(1)} %get-tuple-element.19), channel_id=1, source_target_pairs={{0,12},{1,13},{2,14},{3,15},{4,8},{5,9},{6,10},{7,11},{8,4},{9,5},... | collective-permute-start | bytes 270344 | tf_op jit(solution)/shard_map/ppermute | solution.py:511
  7.7 6.4 %collective-permute-start.3 = (bf16[352,128]{1,0:T(8,128)(2,1)S(1)}, bf16[352,128]{1,0:T(8,128)(2,1)S(1)}, u32[]{:S(2)}, u32[]{:S(2)}) collective-permute-start(bf16[352,128]{1,0:T(8,128)(2,1)S(1)} %get-tuple-element.20), channel_id=1, source_target_pairs={{0,4},{1,5},{2,6},{3,7},{4,0},{5,1},{6,2},{7,3},{8,12},{9,13},{10,... | collective-permute-start | bytes 270344 | tf_op jit(solution)/shard_map/ppermute | solution.py:511
  7.9 30.9 %slice-start = ((s8[18350080]{0:T(1024)(128)(4,1)}), s8[4194304]{0:T(1024)(128)(4,1)S(1)}, s32[]{:S(2)}) async-start(s8[18350080]{0:T(1024)(128)(4,1)} %bitcast), calls=%async_computation.1 | async-start | bytes 8388608
  14.1 24.7 %slice-start.1 = ((s8[18350080]{0:T(1024)(128)(4,1)}), s8[4194304]{0:T(1024)(128)(4,1)S(1)}, s32[]{:S(2)}) async-start(s8[18350080]{0:T(1024)(128)(4,1)} %bitcast), calls=%async_computation.2 | async-start | bytes 8388608
  14.1 24.7 %slice-start.2 = ((s8[18350080]{0:T(1024)(128)(4,1)}), s8[4194304]{0:T(1024)(128)(4,1)S(1)}, s32[]{:S(2)}) async-start(s8[18350080]{0:T(1024)(128)(4,1)} %bitcast), calls=%async_computation.3 | async-start | bytes 8388608
  14.1 24.7 %slice-start.3 = ((s8[18350080]{0:T(1024)(128)(4,1)}), s8[4194304]{0:T(1024)(128)(4,1)S(1)}, s32[]{:S(2)}) async-start(s8[18350080]{0:T(1024)(128)(4,1)} %bitcast), calls=%async_computation.4 | async-start | bytes 8388608
  14.1 24.7 %slice-start.4 = ((s8[18350080]{0:T(1024)(128)(4,1)}), s8[1572864]{0:T(1024)(128)(4,1)S(1)}, s32[]{:S(2)}) async-start(s8[18350080]{0:T(1024)(128)(4,1)} %bitcast), calls=%async_computation.5 | async-start | bytes 3145728
  15.4 1.7 %collective-permute-start.4 = (bf16[64,2688]{1,0:T(8,128)(2,1)S(1)}, bf16[64,2688]{1,0:T(8,128)(2,1)S(1)}, u32[]{:S(2)}, u32[]{:S(2)}) collective-permute-start(bf16[64,2688]{1,0:T(8,128)(2,1)S(1)} %shard_map.140.mine), channel_id=1, source_target_pairs={{0,1},{1,0},{2,3},{3,2},{4,5},{5,4},{6,7},{7,6},{8,9},{9,8},{10,11... | collective-permute-start | bytes 1032200 | tf_op jit(solution)/shard_map/ppermute | solution.py:511
  17.3 8.5 %collective-permute-start.5 = (bf16[64,1792]{1,0:T(8,128)(2,1)S(1)}, bf16[64,1792]{1,0:T(8,128)(2,1)S(1)}, u32[]{:S(2)}, u32[]{:S(2)}) collective-permute-start(bf16[64,1792]{1,0:T(8,128)(2,1)S(1)} %get-tuple-element.22.refs_0_), channel_id=1, source_target_pairs={{0,4},{1,13},{2,6},{3,15},{4,0},{5,9},{6,2},{7,11},{8,12},{9,5},{1... | collective-permute-start | bytes 688136 | tf_op jit(solution)/shard_map/ppermute | solution.py:511
  18.8 10.7 %collective-permute-start.7 = (bf16[32,1792]{1,0:T(8,128)(2,1)S(1)}, bf16[32,1792]{1,0:T(8,128)(2,1)S(1)}, u32[]{:S(2)}, u32[]{:S(2)}) collective-permute-start(bf16[32,1792]{1,0:T(8,128)(2,1)S(1)} %get-tuple-element.23), channel_id=1, source_target_pairs={{0,2},{1,3},{2,0},{3,1},{4,6},{5,7},{6,4},{7,5},{8,10},{9,11},{10,... | collective-permute-start | bytes 344072 | tf_op jit(solution)/shard_map/ppermute | solution.py:511
  25.9 12.3 %collective-permute-start.11 = (bf16[64,1792]{1,0:T(8,128)(2,1)S(1)}, bf16[64,1792]{1,0:T(8,128)(2,1)S(1)}, u32[]{:S(2)}, u32[]{:S(2)}) collective-permute-start(bf16[64,1792]{1,0:T(8,128)(2,1)S(1)} %collective-permute-done.5.refs_1_), channel_id=1, source_target_pairs={{0,16},{1,3},{2,18},{3,1},{4,20},{5,7},{6,22},{7,5},{8,24},{9,11},... | collective-permute-start | bytes 688136 | tf_op jit(solution)/shard_map/ppermute | solution.py:521
  27.5 11.2 %collective-permute-start.9 = (bf16[64,1792]{1,0:T(8,128)(2,1)S(1)}, bf16[64,1792]{1,0:T(8,128)(2,1)S(1)}, u32[]{:S(2)}, u32[]{:S(2)}) collective-permute-start(bf16[64,1792]{1,0:T(8,128)(2,1)S(1)} %collective-permute-done.5.refs_1_), channel_id=1, source_target_pairs={{0,2},{1,5},{2,0},{3,7},{4,6},{5,1},{6,4},{7,3},{8,10},{9,13},{10,... | collective-permute-start | bytes 688136 | tf_op jit(solution)/shard_map/ppermute | solution.py:511
  29.0 9.8 %collective-permute-start.6 = (bf16[64,1792]{1,0:T(8,128)(2,1)S(1)}, bf16[64,1792]{1,0:T(8,128)(2,1)S(1)}, u32[]{:S(2)}, u32[]{:S(2)}) collective-permute-start(bf16[64,1792]{1,0:T(8,128)(2,1)S(1)} %collective-permute-done.5.refs_1_), channel_id=1, source_target_pairs={{0,1},{1,0},{2,3},{3,2},{4,5},{5,4},{6,7},{7,6},{8,9},{9,8},{10,11... | collective-permute-start | bytes 688136 | tf_op jit(solution)/shard_map/ppermute | solution.py:511
  29.0 4.6 %collective-permute-start = (s32[5,64]{1,0:T(8,128)S(1)}, s32[5,64]{1,0:T(8,128)S(1)}, u32[]{:S(2)}, u32[]{:S(2)}) collective-permute-start(s32[5,64]{1,0:T(8,128)S(1)} %get-tuple-element.14.meta.refs_0_), channel_id=1, source_target_pairs={{0,2},{1,3},{2,0},{3,1},{4,6},{5,7},{6,4},{7,5},{8,10},{9,11},{10,... | collective-permute-start | bytes 3848 | tf_op jit(solution)/shard_map/ppermute | solution.py:511
  29.5 8.6 %collective-permute-start.13 = (bf16[32,1792]{1,0:T(8,128)(2,1)S(1)}, bf16[32,1792]{1,0:T(8,128)(2,1)S(1)}, u32[]{:S(2)}, u32[]{:S(2)}) collective-permute-start(bf16[32,1792]{1,0:T(8,128)(2,1)S(1)} %collective-permute-done.7.refs_3_), channel_id=1, source_target_pairs={{0,8},{1,9},{2,10},{3,11},{4,12},{5,13},{6,14},{7,15},{8,0},{9,1},... | collective-permute-start | bytes 344072 | tf_op jit(solution)/shard_map/ppermute | solution.py:511
  33.6 5.2 %collective-permute-start.8 = (bf16[32,1792]{1,0:T(8,128)(2,1)S(1)}, bf16[32,1792]{1,0:T(8,128)(2,1)S(1)}, u32[]{:S(2)}, u32[]{:S(2)}) collective-permute-start(bf16[32,1792]{1,0:T(8,128)(2,1)S(1)} %collective-permute-done.7.refs_3_), channel_id=1, source_target_pairs={{0,1},{1,0},{2,3},{3,2},{4,5},{5,4},{6,7},{7,6},{8,9},{9,8},{10,11... | collective-permute-start | bytes 344072 | tf_op jit(solution)/shard_map/ppermute | solution.py:511
  38.2 6.3 %collective-permute-start.14 = (bf16[32,1792]{1,0:T(8,128)(2,1)S(1)}, bf16[32,1792]{1,0:T(8,128)(2,1)S(1)}, u32[]{:S(2)}, u32[]{:S(2)}) collective-permute-start(bf16[32,1792]{1,0:T(8,128)(2,1)S(1)} %collective-permute-done.13.refs_5_), channel_id=1, source_target_pairs={{0,1},{1,0},{2,3},{3,2},{4,5},{5,4},{6,7},{7,6},{8,9},{9,8},{10,11... | collective-permute-start | bytes 344072 | tf_op jit(solution)/shard_map/ppermute | solution.py:511
  38.2 6.3 %collective-permute-start.12 = (bf16[64,1792]{1,0:T(8,128)(2,1)S(1)}, bf16[64,1792]{1,0:T(8,128)(2,1)S(1)}, u32[]{:S(2)}, u32[]{:S(2)}) collective-permute-start(bf16[64,1792]{1,0:T(8,128)(2,1)S(1)} %collective-permute-done.11.refs_3_), channel_id=1, source_target_pairs={{0,1},{1,0},{2,3},{3,2},{4,5},{5,4},{6,7},{7,6},{8,9},{9,8},{10,11... | collective-permute-start | bytes 688136 | tf_op jit(solution)/shard_map/ppermute | solution.py:511
  38.7 5.8 %collective-permute-start.10 = (bf16[64,1792]{1,0:T(8,128)(2,1)S(1)}, bf16[64,1792]{1,0:T(8,128)(2,1)S(1)}, u32[]{:S(2)}, u32[]{:S(2)}) collective-permute-start(bf16[64,1792]{1,0:T(8,128)(2,1)S(1)} %collective-permute-done.9.refs_1_), channel_id=1, source_target_pairs={{0,1},{1,0},{2,3},{3,2},{4,5},{5,4},{6,7},{7,6},{8,9},{9,8},{10,11... | collective-permute-start | bytes 688136 | tf_op jit(solution)/shard_map/ppermute | solution.py:511

commit v4 on v3

--- a/solution.py
+++ b/solution.py
@@ -166,11 +166,11 @@
     seq_at = lax.axis_index("seq")
     cap = slots.shape[1] // samples
     start = pl.multiple_of(lax.axis_index("vocab") * half, half)
-    moves = [
-        (slots_in, slots), (queries, q_in), (residual.at[:, :, pl.ds(start, half)], r_in),
-    ]
-    for out, flip in zip(outs, flips):
-        taker = jnp.bitwise_xor(seq_at, flip)
+    takers = [jnp.bitwise_xor(seq_at, flip) for flip in flips]
+    moves = [(slots_in, slots)]
+    moves += [(queries.at[taker], q_in.at[n]) for n, taker in enumerate(takers)]
+    moves += [(residual.at[taker, :, pl.ds(start, half)], r_in.at[n]) for n, taker in enumerate(takers)]
+    for out, taker in zip(outs, takers):
         moves.append((keys.at[taker], out.at[pl.ds(0, block), :]))
         moves.append((values.at[taker], out.at[pl.ds(block, block), :]))
     copies = [pltpu.make_async_copy(a, b, sems.at[n]) for n, (a, b) in enumerate(moves)]
@@ -182,16 +182,16 @@
         row = slots[pl.ds(jnp.bitwise_xor(seq_at, flip), 1), :]
         local = jnp.clip(own_slot_column(row, seq_at, cap) - seq_at * block, 0, block - 1)
         onehots.append((iota((cap, block), 1) == local).astype(F32).astype(BF16))
-    first = 2 * block
-    for copy, held in zip(copies[1:3], (q_in, r_in)):
-        copy.wait()
-        for out, flip, onehot in zip(outs, flips, onehots):
-            source = held[jnp.bitwise_xor(seq_at, flip)]
-            picked = jnp.dot(onehot, source, preferred_element_type=F32).astype(BF16)
+    first, at = 2 * block, 1
+    for held in (q_in, r_in):
+        for n, (out, onehot) in enumerate(zip(outs, onehots)):
+            copies[at].wait()
+            at += 1
+            picked = jnp.dot(onehot, held[n], preferred_element_type=F32).astype(BF16)
             for h in range(picked.shape[1] // HD):
                 out[first + h * cap : first + (h + 1) * cap, :] = picked[:, h * HD : (h + 1) * HD]
         first += q_in.shape[2] // HD * cap
-    for copy in copies[3:]:
+    for copy in copies[at:]:
         copy.wait()
 
 
@@ -539,7 +539,7 @@
                 pltpu.VMEM(scored_slots.shape, jnp.int32),
                 pltpu.VMEM(queries.shape, BF16),
                 pltpu.VMEM((samples, block, half_width), BF16),
-                pltpu.SemaphoreType.DMA((3 + 2 * len(flips),)),
+                pltpu.SemaphoreType.DMA((1 + 4 * len(flips),)),
             ],
         )
         far = send(parcels[1], lambda z, x, c: (z ^ 2, x, c))

time: 62.9 us -> 63.5 us (level)
  no operation moved by 1% of the time
where the time goes in v4:
time: 63.5 us; the launch traced here: 63.3 us
  Pallas kernels  19.3 us (30%)
  waiting for transfers between devices  17.2 us (27%)
  starting transfers between devices  14.5 us (23%)
  blocking collectives  11.5 us (18%)
  between operations  0.74 us (1%)
    pallas_call x7, Pallas kernels, call(): pl.pallas_call(body, cost_estimate=cost, out_shape=outs, in_specs=in_spec...  19.3 us
    ppermute x14, waiting for transfers between devices, send(): return lax.ppermute(array, CELL, pairs)  17.2 us
    ppermute x14, starting transfers between devices, send(): return lax.ppermute(array, CELL, pairs)  12.9 us
    all_to_all x1, blocking collectives, steps(): stats = lax.all_to_all(stats, CELL, 0, 0, tiled=True)  11.5 us
    ppermute x1, starting transfers between devices, aside(): return lax.ppermute(array, ('groups',) + CELL, pairs)  1.62 us
  transfers between devices with their start and end apart: 15, of which 6 were waited for; matrix products, arithmetic and copies ran while one was open for 0% of the time, Pallas kernels for 14%

profile of v4, /device:TPU:0, one launch (start us, length us, event | category | flops | bytes accessed | tf_op | source)
XLA Modules:
  0.0 63.3 jit_solution(7150601642487836671)
XLA Ops:
  0.6 2.2 %shard_map.139 = (bf16[352,128]{1,0:T(8,128)(2,1)S(1)}, bf16[352,128]{1,0:T(8,128)(2,1)S(1)}, bf16[352,128]{1,0:T(8,128)(2,1)S(1)}, bf16[352,128]{1,0:T(8,128)(2,1)S(1)}) custom-call(s32[4,64]{1,0:T(4,128)} %slots_in.3, bf16[4,64,128]{2,1,0:T(8,128)(2,1)} %keys.1, bf16[4,64,128]{2,1,0:T(8,128)(2,1)} %values.1, bf16[4,64,896]{2,1,0:T(8,128)(2,1)} %queries.3, ...), custom_call_target="tpu_custom_call" | custom-call | tf_op jit(solution)/shard_map/pallas_call | solution.py:38
  2.8 4.1 %collective-permute-start.1 = (bf16[352,128]{1,0:T(8,128)(2,1)S(1)}, bf16[352,128]{1,0:T(8,128)(2,1)S(1)}, u32[]{:S(2)}, u32[]{:S(2)}) collective-permute-start(bf16[352,128]{1,0:T(8,128)(2,1)S(1)} %get-tuple-element.18), channel_id=1, source_target_pairs={{0,8},{1,9},{2,10},{3,11},{4,12},{5,13},{6,14},{7,15},{8,0},{9,1},... | collective-permute-start | bytes 270344 | tf_op jit(solution)/shard_map/ppermute | solution.py:511
  6.9 1.3 %collective-permute-start.2 = (bf16[352,128]{1,0:T(8,128)(2,1)S(1)}, bf16[352,128]{1,0:T(8,128)(2,1)S(1)}, u32[]{:S(2)}, u32[]{:S(2)}) collective-permute-start(bf16[352,128]{1,0:T(8,128)(2,1)S(1)} %get-tuple-element.19), channel_id=1, source_target_pairs={{0,12},{1,13},{2,14},{3,15},{4,8},{5,9},{6,10},{7,11},{8,4},{9,5},... | collective-permute-start | bytes 270344 | tf_op jit(solution)/shard_map/ppermute | solution.py:511
  8.3 0.2 collective-permute-start.3
  8.5 0.0 slice-start
  8.5 3.3 %shard_map.138 = (s32[4,64]{1,0:T(4,128)S(1)}, bf16[4,112,128]{2,1,0:T(8,128)(2,1)}, bf16[64,1792]{1,0:T(8,128)(2,1)}, s32[5,64]{1,0:T(8,128)S(1)}, bf16[896,179...) custom-call(s32[4,64]{1,0:T(4,128)} %slots_in.3, s32[4,256]{1,0:T(4,128)} %targets_in.1, s32[4]{0:T(128)} %lengths_in.1, ...), custom_call_target="tpu_custom_call" | custom-call | tf_op jit(solution)/shard_map/pallas_call | solution.py:38
  11.8 2.3 %collective-permute-done.1.refs_1_ = bf16[352,128]{1,0:T(8,128)(2,1)S(1)} collective-permute-done((bf16[352,128]{1,0:T(8,128)(2,1)S(1)}, bf16[352,128]{1,0:T(8,128)(2,1)S(1)}, u32[]{:S(2)}, u32[]{:S(2)}) %collective-permute-start.1) | collective-permute-done | bytes 90144 | tf_op jit(solution)/shard_map/ppermute | solution.py:511
  14.2 0.0 collective-permute-done.2.refs_2_
  14.2 0.6 collective-permute-done.3.refs_3_
  14.7 0.0 slice-start.1
  14.7 0.0 slice-start.2
  14.7 0.0 slice-start.3
  14.7 0.0 slice-start.4
  14.7 1.3 %shard_map.140.mine = bf16[64,2688]{1,0:T(8,128)(2,1)S(1)} custom-call(s32[4,64]{1,0:T(4,128)S(1)} %get-tuple-element.15.slots, bf16[896,1792]{1,0:T(8,128)(2,1)S(1)} %get-tuple-element.16.weight, bf16[352,128]{1,0:T(8,128)(2,1)S(1)} %get-tuple-element.17.refs_0_, bf16[352,128]{1,0:T(8,128)(2,1)S(1)} %collective-permute-done.1.refs_1_, ...), custom_call_target="tpu_custom_call" | custom-call | flops 10000000000 | tf_op jit(solution)/shard_map/pallas_call | solution.py:38
  16.0 0.1 collective-permute-start.4
  16.1 1.6 %collective-permute-done.4.other = bf16[64,2688]{1,0:T(8,128)(2,1)S(1)} collective-permute-done((bf16[64,2688]{1,0:T(8,128)(2,1)S(1)}, bf16[64,2688]{1,0:T(8,128)(2,1)S(1)}, u32[]{:S(2)}, u32[]{:S(2)}) %collective-permute-start.4) | collective-permute-done | bytes 344096 | tf_op jit(solution)/shard_map/ppermute | solution.py:511
  17.7 0.2 shard_map.141
  18.0 1.5 %collective-permute-start.5 = (bf16[64,1792]{1,0:T(8,128)(2,1)S(1)}, bf16[64,1792]{1,0:T(8,128)(2,1)S(1)}, u32[]{:S(2)}, u32[]{:S(2)}) collective-permute-start(bf16[64,1792]{1,0:T(8,128)(2,1)S(1)} %get-tuple-element.22.refs_0_), channel_id=1, source_target_pairs={{0,4},{1,13},{2,6},{3,15},{4,0},{5,9},{6,2},{7,11},{8,12},{9,5},{1... | collective-permute-start | bytes 688136 | tf_op jit(solution)/shard_map/ppermute | solution.py:511
  19.4 1.5 %collective-permute-start.7 = (bf16[32,1792]{1,0:T(8,128)(2,1)S(1)}, bf16[32,1792]{1,0:T(8,128)(2,1)S(1)}, u32[]{:S(2)}, u32[]{:S(2)}) collective-permute-start(bf16[32,1792]{1,0:T(8,128)(2,1)S(1)} %get-tuple-element.23), channel_id=1, source_target_pairs={{0,2},{1,3},{2,0},{3,1},{4,6},{5,7},{6,4},{7,5},{8,10},{9,11},{10,... | collective-permute-start | bytes 344072 | tf_op jit(solution)/shard_map/ppermute | solution.py:511
  20.9 5.6 %collective-permute-done.5.refs_1_ = bf16[64,1792]{1,0:T(8,128)(2,1)S(1)} collective-permute-done((bf16[64,1792]{1,0:T(8,128)(2,1)S(1)}, bf16[64,1792]{1,0:T(8,128)(2,1)S(1)}, u32[]{:S(2)}, u32[]{:S(2)}) %collective-permute-start.5) | collective-permute-done | bytes 229408 | tf_op jit(solution)/shard_map/ppermute | solution.py:511
  26.5 1.6 %collective-permute-start.11 = (bf16[64,1792]{1,0:T(8,128)(2,1)S(1)}, bf16[64,1792]{1,0:T(8,128)(2,1)S(1)}, u32[]{:S(2)}, u32[]{:S(2)}) collective-permute-start(bf16[64,1792]{1,0:T(8,128)(2,1)S(1)} %collective-permute-done.5.refs_1_), channel_id=1, source_target_pairs={{0,16},{1,3},{2,18},{3,1},{4,20},{5,7},{6,22},{7,5},{8,24},{9,11},... | collective-permute-start | bytes 688136 | tf_op jit(solution)/shard_map/ppermute | solution.py:521
  28.1 1.5 %collective-permute-start.9 = (bf16[64,1792]{1,0:T(8,128)(2,1)S(1)}, bf16[64,1792]{1,0:T(8,128)(2,1)S(1)}, u32[]{:S(2)}, u32[]{:S(2)}) collective-permute-start(bf16[64,1792]{1,0:T(8,128)(2,1)S(1)} %collective-permute-done.5.refs_1_), channel_id=1, source_target_pairs={{0,2},{1,5},{2,0},{3,7},{4,6},{5,1},{6,4},{7,3},{8,10},{9,13},{10,... | collective-permute-start | bytes 688136 | tf_op jit(solution)/shard_map/ppermute | solution.py:511
  29.6 0.0 collective-permute-start.6
  29.6 0.5 collective-permute-start
  30.2 0.0 collective-permute-done.7.refs_3_
  30.2 1.6 %collective-permute-start.13 = (bf16[32,1792]{1,0:T(8,128)(2,1)S(1)}, bf16[32,1792]{1,0:T(8,128)(2,1)S(1)}, u32[]{:S(2)}, u32[]{:S(2)}) collective-permute-start(bf16[32,1792]{1,0:T(8,128)(2,1)S(1)} %collective-permute-done.7.refs_3_), channel_id=1, source_target_pairs={{0,8},{1,9},{2,10},{3,11},{4,12},{5,13},{6,14},{7,15},{8,0},{9,1},... | collective-permute-start | bytes 344072 | tf_op jit(solution)/shard_map/ppermute | solution.py:511
  31.7 2.5 %collective-permute-done.other_meta.refs_1_ = s32[5,64]{1,0:T(8,128)S(1)} collective-permute-done((s32[5,64]{1,0:T(8,128)S(1)}, s32[5,64]{1,0:T(8,128)S(1)}, u32[]{:S(2)}, u32[]{:S(2)}) %collective-permute-start) | collective-permute-done | bytes 1312 | tf_op jit(solution)/shard_map/ppermute | solution.py:511
  34.2 0.0 collective-permute-start.8
  34.2 4.6 %collective-permute-done.13.refs_5_ = bf16[32,1792]{1,0:T(8,128)(2,1)S(1)} collective-permute-done((bf16[32,1792]{1,0:T(8,128)(2,1)S(1)}, bf16[32,1792]{1,0:T(8,128)(2,1)S(1)}, u32[]{:S(2)}, u32[]{:S(2)}) %collective-permute-start.13) | collective-permute-done | bytes 114720 | tf_op jit(solution)/shard_map/ppermute | solution.py:511
  38.8 0.0 collective-permute-start.14
  38.8 0.0 collective-permute-done.11.refs_3_
  38.8 0.5 collective-permute-start.12
  39.3 0.0 collective-permute-done.9.refs_1_
  39.3 0.1 collective-permute-start.10
  39.4 0.0 collective-permute-done.8.refs_4_
  39.4 0.0 collective-permute-done.6.refs_2_
  39.4 0.0 slice-done
  39.4 0.0 slice-done.1
  39.4 0.0 slice-done.2
  39.4 0.0 slice-done.3
  39.4 0.0 slice-done.4
  39.5 5.6 %shard_map.142.refs_0_ = f32[4,128]{1,0:T(4,128)S(1)} custom-call(bf16[5120,1792]{1,0:T(8,128)(2,1)S(1)} %bitcast.1, s32[5,64]{1,0:T(8,128)S(1)} %get-tuple-element.14.meta.refs_0_, s32[5,64]{1,0:T(8,128)S(1)} %collective-permute-done.other_meta.refs_1_, bf16[64,1792]{1,0:T(8,128)(2,1)S(1)} %get-tuple-element.22.refs_0_, ...), custom_call_target="tpu_custom_call" | custom-call | flops 4697620480 | tf_op jit(solution)/shard_map/pallas_call | solution.py:38
  45.1 0.0 collective-permute-done.14.refs_6_
  45.1 0.0 collective-permute-done.12.refs_4_
  45.1 0.0 collective-permute-done.10.refs_2_
  45.1 5.6 %shard_map.143 = f32[16,8,128]{2,1,0:T(8,128)S(1)} custom-call(bf16[5120,1792]{1,0:T(8,128)(2,1)S(1)} %bitcast.1, s32[5,64]{1,0:T(8,128)S(1)} %get-tuple-element.14.meta.refs_0_, s32[5,64]{1,0:T(8,128)S(1)} %collective-permute-done.other_meta.refs_1_, f32[4,128]{1,0:T(4,128)S(1)} %shard_map.142.refs_0_, bf16[64,1792]{1,0:T(8,128)(2,1)S(1)} %collective-permute-done.9.refs_1_, ...), custom_call_target="tpu_custom_call" | custom-call | flops 4697620480 | tf_op jit(solution)/shard_map/pallas_call | solution.py:38
  50.7 11.5 %all_to_all.5.stats = f32[16,8,128]{2,1,0:T(8,128)S(1)} all-to-all(f32[16,8,128]{2,1,0:T(8,128)S(1)} %shard_map.143), channel_id=1, replica_groups=mesh['groups'=2,'seq'=4,'sample'=2,'vocab'=2] {'seq','sample','vocab'}, dimensions={0} | all-to-all | bytes 131072 | tf_op jit(solution)/shard_map/all_to_all | solution.py:640
  62.2 1.1 %shard_map.144 = (f32[4,16]{1,0:T(4,128)}, f32[4]{0:T(128)}, f32[4]{0:T(128)}, f32[1]{0:T(128)}) custom-call(f32[16,8,128]{2,1,0:T(8,128)S(1)} %all_to_all.5.stats, s32[5,64]{1,0:T(8,128)S(1)} %get-tuple-element.14.meta.refs_0_, s32[5,64]{1,0:T(8,128)S(1)} %collective-permute-done.other_meta.refs_1_), custom_call_target="tpu_custom_call" | custom-call | tf_op jit(solution)/shard_map/pallas_call | solution.py:38
  (1 shorter events, 0.0 us)
Async XLA Ops:
  2.8 11.4 %collective-permute-start.1 = (bf16[352,128]{1,0:T(8,128)(2,1)S(1)}, bf16[352,128]{1,0:T(8,128)(2,1)S(1)}, u32[]{:S(2)}, u32[]{:S(2)}) collective-permute-start(bf16[352,128]{1,0:T(8,128)(2,1)S(1)} %get-tuple-element.18), channel_id=1, source_target_pairs={{0,8},{1,9},{2,10},{3,11},{4,12},{5,13},{6,14},{7,15},{8,0},{9,1},... | collective-permute-start | bytes 270344 | tf_op jit(solution)/shard_map/ppermute | solution.py:511
  6.9 7.2 %collective-permute-start.2 = (bf16[352,128]{1,0:T(8,128)(2,1)S(1)}, bf16[352,128]{1,0:T(8,128)(2,1)S(1)}, u32[]{:S(2)}, u32[]{:S(2)}) collective-permute-start(bf16[352,128]{1,0:T(8,128)(2,1)S(1)} %get-tuple-element.19), channel_id=1, source_target_pairs={{0,12},{1,13},{2,14},{3,15},{4,8},{5,9},{6,10},{7,11},{8,4},{9,5},... | collective-permute-start | bytes 270344 | tf_op jit(solution)/shard_map/ppermute | solution.py:511
  8.3 6.4 %collective-permute-start.3 = (bf16[352,128]{1,0:T(8,128)(2,1)S(1)}, bf16[352,128]{1,0:T(8,128)(2,1)S(1)}, u32[]{:S(2)}, u32[]{:S(2)}) collective-permute-start(bf16[352,128]{1,0:T(8,128)(2,1)S(1)} %get-tuple-element.20), channel_id=1, source_target_pairs={{0,4},{1,5},{2,6},{3,7},{4,0},{5,1},{6,2},{7,3},{8,12},{9,13},{10,... | collective-permute-start | bytes 270344 | tf_op jit(solution)/shard_map/ppermute | solution.py:511
  8.5 30.9 %slice-start = ((s8[18350080]{0:T(1024)(128)(4,1)}), s8[4194304]{0:T(1024)(128)(4,1)S(1)}, s32[]{:S(2)}) async-start(s8[18350080]{0:T(1024)(128)(4,1)} %bitcast), calls=%async_computation.1 | async-start | bytes 8388608
  14.7 24.7 %slice-start.1 = ((s8[18350080]{0:T(1024)(128)(4,1)}), s8[4194304]{0:T(1024)(128)(4,1)S(1)}, s32[]{:S(2)}) async-start(s8[18350080]{0:T(1024)(128)(4,1)} %bitcast), calls=%async_computation.2 | async-start | bytes 8388608
  14.7 24.7 %slice-start.2 = ((s8[18350080]{0:T(1024)(128)(4,1)}), s8[4194304]{0:T(1024)(128)(4,1)S(1)}, s32[]{:S(2)}) async-start(s8[18350080]{0:T(1024)(128)(4,1)} %bitcast), calls=%async_computation.3 | async-start | bytes 8388608
  14.7 24.7 %slice-start.3 = ((s8[18350080]{0:T(1024)(128)(4,1)}), s8[4194304]{0:T(1024)(128)(4,1)S(1)}, s32[]{:S(2)}) async-start(s8[18350080]{0:T(1024)(128)(4,1)} %bitcast), calls=%async_computation.4 | async-start | bytes 8388608
  14.7 24.7 %slice-start.4 = ((s8[18350080]{0:T(1024)(128)(4,1)}), s8[1572864]{0:T(1024)(128)(4,1)S(1)}, s32[]{:S(2)}) async-start(s8[18350080]{0:T(1024)(128)(4,1)} %bitcast), calls=%async_computation.5 | async-start | bytes 3145728
  16.0 1.7 %collective-permute-start.4 = (bf16[64,2688]{1,0:T(8,128)(2,1)S(1)}, bf16[64,2688]{1,0:T(8,128)(2,1)S(1)}, u32[]{:S(2)}, u32[]{:S(2)}) collective-permute-start(bf16[64,2688]{1,0:T(8,128)(2,1)S(1)} %shard_map.140.mine), channel_id=1, source_target_pairs={{0,1},{1,0},{2,3},{3,2},{4,5},{5,4},{6,7},{7,6},{8,9},{9,8},{10,11... | collective-permute-start | bytes 1032200 | tf_op jit(solution)/shard_map/ppermute | solution.py:511
  18.0 8.5 %collective-permute-start.5 = (bf16[64,1792]{1,0:T(8,128)(2,1)S(1)}, bf16[64,1792]{1,0:T(8,128)(2,1)S(1)}, u32[]{:S(2)}, u32[]{:S(2)}) collective-permute-start(bf16[64,1792]{1,0:T(8,128)(2,1)S(1)} %get-tuple-element.22.refs_0_), channel_id=1, source_target_pairs={{0,4},{1,13},{2,6},{3,15},{4,0},{5,9},{6,2},{7,11},{8,12},{9,5},{1... | collective-permute-start | bytes 688136 | tf_op jit(solution)/shard_map/ppermute | solution.py:511
  19.4 10.7 %collective-permute-start.7 = (bf16[32,1792]{1,0:T(8,128)(2,1)S(1)}, bf16[32,1792]{1,0:T(8,128)(2,1)S(1)}, u32[]{:S(2)}, u32[]{:S(2)}) collective-permute-start(bf16[32,1792]{1,0:T(8,128)(2,1)S(1)} %get-tuple-element.23), channel_id=1, source_target_pairs={{0,2},{1,3},{2,0},{3,1},{4,6},{5,7},{6,4},{7,5},{8,10},{9,11},{10,... | collective-permute-start | bytes 344072 | tf_op jit(solution)/shard_map/ppermute | solution.py:511
  26.5 12.3 %collective-permute-start.11 = (bf16[64,1792]{1,0:T(8,128)(2,1)S(1)}, bf16[64,1792]{1,0:T(8,128)(2,1)S(1)}, u32[]{:S(2)}, u32[]{:S(2)}) collective-permute-start(bf16[64,1792]{1,0:T(8,128)(2,1)S(1)} %collective-permute-done.5.refs_1_), channel_id=1, source_target_pairs={{0,16},{1,3},{2,18},{3,1},{4,20},{5,7},{6,22},{7,5},{8,24},{9,11},... | collective-permute-start | bytes 688136 | tf_op jit(solution)/shard_map/ppermute | solution.py:521
  28.1 11.2 %collective-permute-start.9 = (bf16[64,1792]{1,0:T(8,128)(2,1)S(1)}, bf16[64,1792]{1,0:T(8,128)(2,1)S(1)}, u32[]{:S(2)}, u32[]{:S(2)}) collective-permute-start(bf16[64,1792]{1,0:T(8,128)(2,1)S(1)} %collective-permute-done.5.refs_1_), channel_id=1, source_target_pairs={{0,2},{1,5},{2,0},{3,7},{4,6},{5,1},{6,4},{7,3},{8,10},{9,13},{10,... | collective-permute-start | bytes 688136 | tf_op jit(solution)/shard_map/ppermute | solution.py:511
  29.6 9.8 %collective-permute-start.6 = (bf16[64,1792]{1,0:T(8,128)(2,1)S(1)}, bf16[64,1792]{1,0:T(8,128)(2,1)S(1)}, u32[]{:S(2)}, u32[]{:S(2)}) collective-permute-start(bf16[64,1792]{1,0:T(8,128)(2,1)S(1)} %collective-permute-done.5.refs_1_), channel_id=1, source_target_pairs={{0,1},{1,0},{2,3},{3,2},{4,5},{5,4},{6,7},{7,6},{8,9},{9,8},{10,11... | collective-permute-start | bytes 688136 | tf_op jit(solution)/shard_map/ppermute | solution.py:511
  29.6 4.6 %collective-permute-start = (s32[5,64]{1,0:T(8,128)S(1)}, s32[5,64]{1,0:T(8,128)S(1)}, u32[]{:S(2)}, u32[]{:S(2)}) collective-permute-start(s32[5,64]{1,0:T(8,128)S(1)} %get-tuple-element.14.meta.refs_0_), channel_id=1, source_target_pairs={{0,2},{1,3},{2,0},{3,1},{4,6},{5,7},{6,4},{7,5},{8,10},{9,11},{10,... | collective-permute-start | bytes 3848 | tf_op jit(solution)/shard_map/ppermute | solution.py:511
  30.2 8.6 %collective-permute-start.13 = (bf16[32,1792]{1,0:T(8,128)(2,1)S(1)}, bf16[32,1792]{1,0:T(8,128)(2,1)S(1)}, u32[]{:S(2)}, u32[]{:S(2)}) collective-permute-start(bf16[32,1792]{1,0:T(8,128)(2,1)S(1)} %collective-permute-done.7.refs_3_), channel_id=1, source_target_pairs={{0,8},{1,9},{2,10},{3,11},{4,12},{5,13},{6,14},{7,15},{8,0},{9,1},... | collective-permute-start | bytes 344072 | tf_op jit(solution)/shard_map/ppermute | solution.py:511
  34.2 5.2 %collective-permute-start.8 = (bf16[32,1792]{1,0:T(8,128)(2,1)S(1)}, bf16[32,1792]{1,0:T(8,128)(2,1)S(1)}, u32[]{:S(2)}, u32[]{:S(2)}) collective-permute-start(bf16[32,1792]{1,0:T(8,128)(2,1)S(1)} %collective-permute-done.7.refs_3_), channel_id=1, source_target_pairs={{0,1},{1,0},{2,3},{3,2},{4,5},{5,4},{6,7},{7,6},{8,9},{9,8},{10,11... | collective-permute-start | bytes 344072 | tf_op jit(solution)/shard_map/ppermute | solution.py:511
  38.8 6.3 %collective-permute-start.14 = (bf16[32,1792]{1,0:T(8,128)(2,1)S(1)}, bf16[32,1792]{1,0:T(8,128)(2,1)S(1)}, u32[]{:S(2)}, u32[]{:S(2)}) collective-permute-start(bf16[32,1792]{1,0:T(8,128)(2,1)S(1)} %collective-permute-done.13.refs_5_), channel_id=1, source_target_pairs={{0,1},{1,0},{2,3},{3,2},{4,5},{5,4},{6,7},{7,6},{8,9},{9,8},{10,11... | collective-permute-start | bytes 344072 | tf_op jit(solution)/shard_map/ppermute | solution.py:511
  38.8 6.3 %collective-permute-start.12 = (bf16[64,1792]{1,0:T(8,128)(2,1)S(1)}, bf16[64,1792]{1,0:T(8,128)(2,1)S(1)}, u32[]{:S(2)}, u32[]{:S(2)}) collective-permute-start(bf16[64,1792]{1,0:T(8,128)(2,1)S(1)} %collective-permute-done.11.refs_3_), channel_id=1, source_target_pairs={{0,1},{1,0},{2,3},{3,2},{4,5},{5,4},{6,7},{7,6},{8,9},{9,8},{10,11... | collective-permute-start | bytes 688136 | tf_op jit(solution)/shard_map/ppermute | solution.py:511
  39.3 5.8 %collective-permute-start.10 = (bf16[64,1792]{1,0:T(8,128)(2,1)S(1)}, bf16[64,1792]{1,0:T(8,128)(2,1)S(1)}, u32[]{:S(2)}, u32[]{:S(2)}) collective-permute-start(bf16[64,1792]{1,0:T(8,128)(2,1)S(1)} %collective-permute-done.9.refs_1_), channel_id=1, source_target_pairs={{0,1},{1,0},{2,3},{3,2},{4,5},{5,4},{6,7},{7,6},{8,9},{9,8},{10,11... | collective-permute-start | bytes 688136 | tf_op jit(solution)/shard_map/ppermute | solution.py:511
